TPU v7x, 32 devices: a 4x2x2 block of a 4x4x8 slice. The times are simulated.
32 devices in a mesh: dp: 4 (over y, z), cp: 8 (over x, core).
Axes of the slice: x: 4, y: 2, z: 2, core: 2. Of those that a mesh axis runs over, the one named last changes fastest.
The devices are a block of a 4x4x8 slice.
Arguments:
- latents: bfloat16 [8, 128, 128, 16], P('dp', 'cp'), parts along dimension 0
- w_in: bfloat16 [3, 3, 16, 512], replicated
- b_in: bfloat16 [512], replicated
- w_conv: bfloat16 [4, 3, 3, 512, 512], replicated
- b_conv: bfloat16 [4, 512], replicated
- gn_scale: bfloat16 [5, 512], replicated
- gn_shift: bfloat16 [5, 512], replicated
- w_attn: bfloat16 [4, 512, 512], replicated
- b_attn: bfloat16 [4, 512], replicated
Outputs:
- output: bfloat16 [8, 128, 128, 512], P('dp', 'cp'), parts along dimension 0
There are 4 independent parts. A program takes and returns all parts, laid end to end along the dimension named above; an argument that names none is the same for every part.
All inputs are finite; a program needn't handle non-finite values.
Results may differ from a plain program's by a relative error of at most 0.02.
Values are sent between devices in bfloat16 or wider.
A program may use at most 768 MiB of HBM per device.

v0:
```python
import jax
import jax.numpy as jnp
from jax import lax
from jax.sharding import PartitionSpec as P

GROUPS = 32
GN_EPS = 1e-6
QUERY_TOKENS = 512


def group_norm(x_val, norm_gain, norm_bias, n_dev):
    n_batch, n_rows, n_width, n_chan = x_val.shape
    grouped = x_val.reshape(n_batch, n_rows, n_width, GROUPS, n_chan // GROUPS)
    local_sums = jnp.stack([jnp.sum(grouped, axis=(1, 2, 4), dtype=jnp.float32), jnp.sum(jnp.square(grouped.astype(jnp.float32)), axis=(1, 2, 4))])
    totals = lax.psum(local_sums, 'cp')
    elem_count = n_rows * n_width * (n_chan // GROUPS) * n_dev
    grp_mean = totals[0] / elem_count
    inv_std = lax.rsqrt(totals[1] / elem_count - jnp.square(grp_mean) + GN_EPS)
    normed = (grouped - grp_mean[:, None, None, :, None]) * inv_std[:, None, None, :, None]
    return normed.reshape(x_val.shape) * norm_gain + norm_bias


def conv_rows(x_val, weight, conv_bias, n_dev):
    down_pairs = [(sender, sender + 1) for sender in range(n_dev - 1)]
    up_pairs = [(sender + 1, sender) for sender in range(n_dev - 1)]
    from_above = lax.ppermute(x_val[:, -1:], 'cp', down_pairs)
    from_below = lax.ppermute(x_val[:, :1], 'cp', up_pairs)
    padded = jnp.concatenate([from_above, x_val, from_below], axis=1)
    conv_out = lax.conv_general_dilated(padded, weight, (1, 1), ((0, 0), (1, 1)), dimension_numbers=('NHWC', 'HWIO', 'NHWC'), preferred_element_type=jnp.float32)
    return conv_out + conv_bias


def resnet_block(h_val, w_conv, b_conv, gn_scale, gn_shift, conv_idx, norm_idx, n_dev):
    act_in = jax.nn.silu(group_norm(h_val, gn_scale[norm_idx], gn_shift[norm_idx], n_dev)).astype(jnp.bfloat16)
    mid_act = conv_rows(act_in, w_conv[conv_idx], b_conv[conv_idx], n_dev).astype(jnp.bfloat16)
    act_two = jax.nn.silu(group_norm(mid_act, gn_scale[norm_idx + 1], gn_shift[norm_idx + 1], n_dev)).astype(jnp.bfloat16)
    conv_two = conv_rows(act_two, w_conv[conv_idx + 1], b_conv[conv_idx + 1], n_dev)
    return (h_val + conv_two).astype(jnp.bfloat16)


def attend(queries, keys_all, vals_all):
    n_batch, n_query, n_chan = queries.shape
    block_len = max([divisor for divisor in range(1, min(n_query, QUERY_TOKENS) + 1) if n_query % divisor == 0])
    n_blocks = n_query // block_len
    q_blocks = queries.reshape(n_batch * n_blocks, block_len, n_chan)
    att_scale = n_chan ** -0.5

    def attend_step(step_idx, out_buf):
        q_block = lax.dynamic_index_in_dim(q_blocks, step_idx, 0, keepdims=False)
        sample_idx = step_idx // n_blocks
        k_sample = lax.dynamic_index_in_dim(keys_all, sample_idx, 0, keepdims=False)
        v_sample = lax.dynamic_index_in_dim(vals_all, sample_idx, 0, keepdims=False)
        scores = lax.dot_general(q_block, k_sample, (((1,), (1,)), ((), ())), preferred_element_type=jnp.float32) * att_scale
        attn_prob = jax.nn.softmax(scores, axis=-1).astype(jnp.bfloat16)
        o_block = jnp.dot(attn_prob, v_sample, preferred_element_type=jnp.float32).astype(jnp.bfloat16)
        return lax.dynamic_update_index_in_dim(out_buf, o_block, step_idx, 0)

    attended = lax.fori_loop(0, n_batch * n_blocks, attend_step, jnp.zeros_like(q_blocks))
    return attended.reshape(n_batch, n_query, n_chan)


def solution(mesh):
    n_dev = mesh.shape['cp']

    def local_fn(latents, w_in, b_in, w_conv, b_conv, gn_scale, gn_shift, w_attn, b_attn):
        hidden = conv_rows(latents, w_in, b_in, n_dev).astype(jnp.bfloat16)
        hidden = resnet_block(hidden, w_conv, b_conv, gn_scale, gn_shift, 0, 0, n_dev)
        n_batch, n_rows, n_width, n_chan = hidden.shape
        normed = group_norm(hidden, gn_scale[2], gn_shift[2], n_dev).astype(jnp.bfloat16).reshape(-1, n_chan)

        def project(j_idx):
            proj = jnp.dot(normed, w_attn[j_idx], preferred_element_type=jnp.float32) + b_attn[j_idx]
            return proj.astype(jnp.bfloat16).reshape(n_batch, n_rows * n_width, n_chan)

        keys_all = lax.all_gather(project(1), 'cp', axis=1, tiled=True)
        vals_all = lax.all_gather(project(2), 'cp', axis=1, tiled=True)
        attended = attend(project(0), keys_all, vals_all).reshape(-1, n_chan)
        proj_out = jnp.dot(attended, w_attn[3], preferred_element_type=jnp.float32) + b_attn[3]
        hidden = (hidden + proj_out.reshape(hidden.shape)).astype(jnp.bfloat16)
        return resnet_block(hidden, w_conv, b_conv, gn_scale, gn_shift, 2, 3, n_dev)

    band_spec = P('dp', 'cp')
    whole_spec = P()
    return jax.shard_map(local_fn, mesh=mesh, in_specs=(band_spec,) + (whole_spec,) * 8, out_specs=band_spec, check_vma=False)
```

profile of v0, /device:TPU:81, one launch (start us, length us, event | category | flops | bytes accessed | tf_op | source)
XLA Modules:
  0.0 1325.9 jit_solution(11105778560602432492)
XLA Ops:
  27.1 7.5 convert_multiply_fusion.1
  40.0 8.7 copy.60
  49.5 12.8 psum.35
  64.9 11.7 multiply_convert_fusion.2
  92.5 6.1 maximum_bitcast_fusion
  98.5 9.9 copy.104
  108.4 9.8 pad.2.clone
  119.6 6.3 fusion.47
  125.9 26.7 %convert_multiply_fusion.4 = (f32[16,16,17,512]{3,1,2,0:T(8,128)}, bf16[16,16,17,512]{3,1,2,0:T(8,128)(2,1)S(1)}) fusion(f32[512]{0:T(512)S(1)} %bitcast.336, bf16[4,3,3,512,512]{4,3,2,1,0:T(8,128)(2,1)} %param.14, bf16[18,2,8,19,512]{4,1,3,2,0:T(2,128)(2,1)S(1)} %fusion.47, pred[16,17]{0,1:T(8,128)(4,1)S(1)} %copy-done.24), kind=kOutput, calls=%fused_computation.110 | convolution fusion | flops 20546453504 | bytes 23693584 | tf_op jit(solution)/shard_map/conv_general_dilated | solution.py:29
  158.0 8.7 copy.71
  167.4 11.4 psum.36
  181.4 11.7 multiply_convert_fusion.1
  214.8 9.9 copy.105
  224.7 9.8 pad.4.clone
  236.0 6.4 fusion.48
  242.4 27.3 %convert_multiply_fusion.3 = (f32[16,16,17,512]{3,1,2,0:T(8,128)}, bf16[16,16,17,512]{3,1,2,0:T(8,128)(2,1)S(1)}) fusion(f32[512]{0:T(512)S(1)} %bitcast.335, bf16[4,3,3,512,512]{4,3,2,1,0:T(8,128)(2,1)} %param.14, bf16[18,2,8,19,512]{4,1,3,2,0:T(2,128)(2,1)S(1)} %fusion.48, pred[16,17]{0,1:T(8,128)(4,1)S(1)} %copy-done.24, ...), kind=kOutput, calls=%fused_computation.109 | convolution fusion | flops 20550909952 | bytes 28150032 | tf_op jit(solution)/shard_map/conv_general_dilated | solution.py:29
  278.6 8.7 copy.82
  288.0 11.5 psum.37
  302.3 11.6 fusion.29
  326.0 6.5 add_convert_fusion.4
  332.5 6.5 add_convert_fusion.6
  339.0 142.9 %all-gather.3.cloned.1.call-done = bf16[2,16384,512]{2,1,0:T(8,128)(2,1)} async-done(((bf16[2,2048,512]{2,1,0:T(8,128)(2,1)}), bf16[2,16384,512]{2,1,0:T(8,128)(2,1)}) %all-gather.3.cloned.1.call-update) | async-done | bytes 33554448 | tf_op jit(solution)/shard_map/all_gather | solution.py:75
  481.9 156.2 %all-gather.5.cloned.1.call-done = bf16[2,16384,512]{2,1,0:T(8,128)(2,1)} async-done(((bf16[2,2048,512]{2,1,0:T(8,128)(2,1)}), bf16[2,16384,512]{2,1,0:T(8,128)(2,1)}) %all-gather.5.cloned.1.call-update) | async-done | bytes 33554448 | tf_op jit(solution)/shard_map/all_gather | solution.py:76
  638.1 443.5 %while.15 = (s32[]{:T(128)}, bf16[8,512,512]{2,1,0:T(8,128)(2,1)}, bf16[8,512,512]{2,1,0:T(8,128)(2,1)}, bf16[2,16384,512]{2,1,0:T(8,128)(2,1)}, bf16[2,16384,51...) while((s32[]{:T(128)}, bf16[8,512,512]{2,1,0:T(8,128)(2,1)}, ...), condition=%wide.region_18.19_spmd, body=%wide.region_15.18_spmd.sunk | while | flops 17255628800 | bytes 135277792 | solution.py:58
  638.5 19.9 %multiply_reduce_fusion.2 = (f32[512]{0:T(512)S(1)}, f32[512,16384]{1,0:T(8,128)}) fusion(bf16[2,16384,512]{2,1,0:T(8,128)(2,1)} %get-tuple-element.248, s32[]{:T(128)S(6)} %select_n.38, bf16[8,512,512]{2,1,0:T(8,128)(2,1)} %get-tuple-element.247, s32[]{:T(128)} %get-tuple-element.235), kind=kOutput, calls=%fused_computation.2.clone.1 | convolution fusion | flops 8606711808 | bytes 50858500 | tf_op jit(solution)/shard_map/while/body/eval_jaxpr/dot_general | solution.py:53
  658.5 14.1 %fusion.138 = f32[512]{0:T(512)S(1)} fusion(f32[512,16384]{1,0:T(8,128)} %get-tuple-element.223, f32[512]{0:T(512)S(1)} %get-tuple-element.224), kind=kLoop, calls=%fused_computation.3.clone.1 | loop fusion | flops 25165312 | bytes 33558528 | tf_op jit(solution)/shard_map/while/body/eval_jaxpr/reduce_sum | solution.py:54
  672.5 21.4 %fusion.139 = bf16[8,512,512]{2,1,0:T(8,128)(2,1)} fusion(bf16[8,512,512]{2,1,0:T(8,128)(2,1)} %get-tuple-element.236, s32[]{:T(128)} %get-tuple-element.235, bf16[2,16384,512]{2,1,0:T(8,128)(2,1)} %get-tuple-element.249, s32[]{:T(128)S(6)} %select_n.38, f32[512,16384]{1,0:T(8,128)} %get-tuple-element.223, f32[512]{0:T(512)S(1)} %fusion.138, ...), kind=kOutput, calls=%fused_computation.12.clone.1 | convolution fusion | flops 8623751168 | bytes 50860548 | tf_op jit(solution)/shard_map/while/body/eval_jaxpr/dot_general | solution.py:55
  694.0 19.9 %multiply_reduce_fusion.2 = (f32[512]{0:T(512)S(1)}, f32[512,16384]{1,0:T(8,128)}) fusion(bf16[2,16384,512]{2,1,0:T(8,128)(2,1)} %get-tuple-element.248, s32[]{:T(128)S(6)} %select_n.38, bf16[8,512,512]{2,1,0:T(8,128)(2,1)} %get-tuple-element.247, s32[]{:T(128)} %get-tuple-element.235), kind=kOutput, calls=%fused_computation.2.clone.1 | convolution fusion | flops 8606711808 | bytes 50858500 | tf_op jit(solution)/shard_map/while/body/eval_jaxpr/dot_general | solution.py:53
  713.8 14.1 %fusion.138 = f32[512]{0:T(512)S(1)} fusion(f32[512,16384]{1,0:T(8,128)} %get-tuple-element.223, f32[512]{0:T(512)S(1)} %get-tuple-element.224), kind=kLoop, calls=%fused_computation.3.clone.1 | loop fusion | flops 25165312 | bytes 33558528 | tf_op jit(solution)/shard_map/while/body/eval_jaxpr/reduce_sum | solution.py:54
  727.9 21.4 %fusion.139 = bf16[8,512,512]{2,1,0:T(8,128)(2,1)} fusion(bf16[8,512,512]{2,1,0:T(8,128)(2,1)} %get-tuple-element.236, s32[]{:T(128)} %get-tuple-element.235, bf16[2,16384,512]{2,1,0:T(8,128)(2,1)} %get-tuple-element.249, s32[]{:T(128)S(6)} %select_n.38, f32[512,16384]{1,0:T(8,128)} %get-tuple-element.223, f32[512]{0:T(512)S(1)} %fusion.138, ...), kind=kOutput, calls=%fused_computation.12.clone.1 | convolution fusion | flops 8623751168 | bytes 50860548 | tf_op jit(solution)/shard_map/while/body/eval_jaxpr/dot_general | solution.py:55
  749.3 19.9 %multiply_reduce_fusion.2 = (f32[512]{0:T(512)S(1)}, f32[512,16384]{1,0:T(8,128)}) fusion(bf16[2,16384,512]{2,1,0:T(8,128)(2,1)} %get-tuple-element.248, s32[]{:T(128)S(6)} %select_n.38, bf16[8,512,512]{2,1,0:T(8,128)(2,1)} %get-tuple-element.247, s32[]{:T(128)} %get-tuple-element.235), kind=kOutput, calls=%fused_computation.2.clone.1 | convolution fusion | flops 8606711808 | bytes 50858500 | tf_op jit(solution)/shard_map/while/body/eval_jaxpr/dot_general | solution.py:53
  769.2 14.1 %fusion.138 = f32[512]{0:T(512)S(1)} fusion(f32[512,16384]{1,0:T(8,128)} %get-tuple-element.223, f32[512]{0:T(512)S(1)} %get-tuple-element.224), kind=kLoop, calls=%fused_computation.3.clone.1 | loop fusion | flops 25165312 | bytes 33558528 | tf_op jit(solution)/shard_map/while/body/eval_jaxpr/reduce_sum | solution.py:54
  783.3 21.4 %fusion.139 = bf16[8,512,512]{2,1,0:T(8,128)(2,1)} fusion(bf16[8,512,512]{2,1,0:T(8,128)(2,1)} %get-tuple-element.236, s32[]{:T(128)} %get-tuple-element.235, bf16[2,16384,512]{2,1,0:T(8,128)(2,1)} %get-tuple-element.249, s32[]{:T(128)S(6)} %select_n.38, f32[512,16384]{1,0:T(8,128)} %get-tuple-element.223, f32[512]{0:T(512)S(1)} %fusion.138, ...), kind=kOutput, calls=%fused_computation.12.clone.1 | convolution fusion | flops 8623751168 | bytes 50860548 | tf_op jit(solution)/shard_map/while/body/eval_jaxpr/dot_general | solution.py:55
  804.7 19.9 %multiply_reduce_fusion.2 = (f32[512]{0:T(512)S(1)}, f32[512,16384]{1,0:T(8,128)}) fusion(bf16[2,16384,512]{2,1,0:T(8,128)(2,1)} %get-tuple-element.248, s32[]{:T(128)S(6)} %select_n.38, bf16[8,512,512]{2,1,0:T(8,128)(2,1)} %get-tuple-element.247, s32[]{:T(128)} %get-tuple-element.235), kind=kOutput, calls=%fused_computation.2.clone.1 | convolution fusion | flops 8606711808 | bytes 50858500 | tf_op jit(solution)/shard_map/while/body/eval_jaxpr/dot_general | solution.py:53
  824.6 14.1 %fusion.138 = f32[512]{0:T(512)S(1)} fusion(f32[512,16384]{1,0:T(8,128)} %get-tuple-element.223, f32[512]{0:T(512)S(1)} %get-tuple-element.224), kind=kLoop, calls=%fused_computation.3.clone.1 | loop fusion | flops 25165312 | bytes 33558528 | tf_op jit(solution)/shard_map/while/body/eval_jaxpr/reduce_sum | solution.py:54
  838.7 21.4 %fusion.139 = bf16[8,512,512]{2,1,0:T(8,128)(2,1)} fusion(bf16[8,512,512]{2,1,0:T(8,128)(2,1)} %get-tuple-element.236, s32[]{:T(128)} %get-tuple-element.235, bf16[2,16384,512]{2,1,0:T(8,128)(2,1)} %get-tuple-element.249, s32[]{:T(128)S(6)} %select_n.38, f32[512,16384]{1,0:T(8,128)} %get-tuple-element.223, f32[512]{0:T(512)S(1)} %fusion.138, ...), kind=kOutput, calls=%fused_computation.12.clone.1 | convolution fusion | flops 8623751168 | bytes 50860548 | tf_op jit(solution)/shard_map/while/body/eval_jaxpr/dot_general | solution.py:55
  860.1 19.9 %multiply_reduce_fusion.2 = (f32[512]{0:T(512)S(1)}, f32[512,16384]{1,0:T(8,128)}) fusion(bf16[2,16384,512]{2,1,0:T(8,128)(2,1)} %get-tuple-element.248, s32[]{:T(128)S(6)} %select_n.38, bf16[8,512,512]{2,1,0:T(8,128)(2,1)} %get-tuple-element.247, s32[]{:T(128)} %get-tuple-element.235), kind=kOutput, calls=%fused_computation.2.clone.1 | convolution fusion | flops 8606711808 | bytes 50858500 | tf_op jit(solution)/shard_map/while/body/eval_jaxpr/dot_general | solution.py:53
  880.0 14.1 %fusion.138 = f32[512]{0:T(512)S(1)} fusion(f32[512,16384]{1,0:T(8,128)} %get-tuple-element.223, f32[512]{0:T(512)S(1)} %get-tuple-element.224), kind=kLoop, calls=%fused_computation.3.clone.1 | loop fusion | flops 25165312 | bytes 33558528 | tf_op jit(solution)/shard_map/while/body/eval_jaxpr/reduce_sum | solution.py:54
  894.1 21.4 %fusion.139 = bf16[8,512,512]{2,1,0:T(8,128)(2,1)} fusion(bf16[8,512,512]{2,1,0:T(8,128)(2,1)} %get-tuple-element.236, s32[]{:T(128)} %get-tuple-element.235, bf16[2,16384,512]{2,1,0:T(8,128)(2,1)} %get-tuple-element.249, s32[]{:T(128)S(6)} %select_n.38, f32[512,16384]{1,0:T(8,128)} %get-tuple-element.223, f32[512]{0:T(512)S(1)} %fusion.138, ...), kind=kOutput, calls=%fused_computation.12.clone.1 | convolution fusion | flops 8623751168 | bytes 50860548 | tf_op jit(solution)/shard_map/while/body/eval_jaxpr/dot_general | solution.py:55
  915.5 19.9 %multiply_reduce_fusion.2 = (f32[512]{0:T(512)S(1)}, f32[512,16384]{1,0:T(8,128)}) fusion(bf16[2,16384,512]{2,1,0:T(8,128)(2,1)} %get-tuple-element.248, s32[]{:T(128)S(6)} %select_n.38, bf16[8,512,512]{2,1,0:T(8,128)(2,1)} %get-tuple-element.247, s32[]{:T(128)} %get-tuple-element.235), kind=kOutput, calls=%fused_computation.2.clone.1 | convolution fusion | flops 8606711808 | bytes 50858500 | tf_op jit(solution)/shard_map/while/body/eval_jaxpr/dot_general | solution.py:53
  935.4 14.1 %fusion.138 = f32[512]{0:T(512)S(1)} fusion(f32[512,16384]{1,0:T(8,128)} %get-tuple-element.223, f32[512]{0:T(512)S(1)} %get-tuple-element.224), kind=kLoop, calls=%fused_computation.3.clone.1 | loop fusion | flops 25165312 | bytes 33558528 | tf_op jit(solution)/shard_map/while/body/eval_jaxpr/reduce_sum | solution.py:54
  949.4 21.4 %fusion.139 = bf16[8,512,512]{2,1,0:T(8,128)(2,1)} fusion(bf16[8,512,512]{2,1,0:T(8,128)(2,1)} %get-tuple-element.236, s32[]{:T(128)} %get-tuple-element.235, bf16[2,16384,512]{2,1,0:T(8,128)(2,1)} %get-tuple-element.249, s32[]{:T(128)S(6)} %select_n.38, f32[512,16384]{1,0:T(8,128)} %get-tuple-element.223, f32[512]{0:T(512)S(1)} %fusion.138, ...), kind=kOutput, calls=%fused_computation.12.clone.1 | convolution fusion | flops 8623751168 | bytes 50860548 | tf_op jit(solution)/shard_map/while/body/eval_jaxpr/dot_general | solution.py:55
  970.9 19.9 %multiply_reduce_fusion.2 = (f32[512]{0:T(512)S(1)}, f32[512,16384]{1,0:T(8,128)}) fusion(bf16[2,16384,512]{2,1,0:T(8,128)(2,1)} %get-tuple-element.248, s32[]{:T(128)S(6)} %select_n.38, bf16[8,512,512]{2,1,0:T(8,128)(2,1)} %get-tuple-element.247, s32[]{:T(128)} %get-tuple-element.235), kind=kOutput, calls=%fused_computation.2.clone.1 | convolution fusion | flops 8606711808 | bytes 50858500 | tf_op jit(solution)/shard_map/while/body/eval_jaxpr/dot_general | solution.py:53
  990.8 14.1 %fusion.138 = f32[512]{0:T(512)S(1)} fusion(f32[512,16384]{1,0:T(8,128)} %get-tuple-element.223, f32[512]{0:T(512)S(1)} %get-tuple-element.224), kind=kLoop, calls=%fused_computation.3.clone.1 | loop fusion | flops 25165312 | bytes 33558528 | tf_op jit(solution)/shard_map/while/body/eval_jaxpr/reduce_sum | solution.py:54
  1004.8 21.4 %fusion.139 = bf16[8,512,512]{2,1,0:T(8,128)(2,1)} fusion(bf16[8,512,512]{2,1,0:T(8,128)(2,1)} %get-tuple-element.236, s32[]{:T(128)} %get-tuple-element.235, bf16[2,16384,512]{2,1,0:T(8,128)(2,1)} %get-tuple-element.249, s32[]{:T(128)S(6)} %select_n.38, f32[512,16384]{1,0:T(8,128)} %get-tuple-element.223, f32[512]{0:T(512)S(1)} %fusion.138, ...), kind=kOutput, calls=%fused_computation.12.clone.1 | convolution fusion | flops 8623751168 | bytes 50860548 | tf_op jit(solution)/shard_map/while/body/eval_jaxpr/dot_general | solution.py:55
  1026.2 19.9 %multiply_reduce_fusion.2 = (f32[512]{0:T(512)S(1)}, f32[512,16384]{1,0:T(8,128)}) fusion(bf16[2,16384,512]{2,1,0:T(8,128)(2,1)} %get-tuple-element.248, s32[]{:T(128)S(6)} %select_n.38, bf16[8,512,512]{2,1,0:T(8,128)(2,1)} %get-tuple-element.247, s32[]{:T(128)} %get-tuple-element.235), kind=kOutput, calls=%fused_computation.2.clone.1 | convolution fusion | flops 8606711808 | bytes 50858500 | tf_op jit(solution)/shard_map/while/body/eval_jaxpr/dot_general | solution.py:53
  1046.1 14.1 %fusion.138 = f32[512]{0:T(512)S(1)} fusion(f32[512,16384]{1,0:T(8,128)} %get-tuple-element.223, f32[512]{0:T(512)S(1)} %get-tuple-element.224), kind=kLoop, calls=%fused_computation.3.clone.1 | loop fusion | flops 25165312 | bytes 33558528 | tf_op jit(solution)/shard_map/while/body/eval_jaxpr/reduce_sum | solution.py:54
  1060.2 21.4 %fusion.139 = bf16[8,512,512]{2,1,0:T(8,128)(2,1)} fusion(bf16[8,512,512]{2,1,0:T(8,128)(2,1)} %get-tuple-element.236, s32[]{:T(128)} %get-tuple-element.235, bf16[2,16384,512]{2,1,0:T(8,128)(2,1)} %get-tuple-element.249, s32[]{:T(128)S(6)} %select_n.38, f32[512,16384]{1,0:T(8,128)} %get-tuple-element.223, f32[512]{0:T(512)S(1)} %fusion.138, ...), kind=kOutput, calls=%fused_computation.12.clone.1 | convolution fusion | flops 8623751168 | bytes 50860548 | tf_op jit(solution)/shard_map/while/body/eval_jaxpr/dot_general | solution.py:55
  1086.6 6.7 convert_reduce_fusion
  1093.7 12.1 psum.38
  1130.1 9.9 copy.106
  1139.9 9.8 pad.6.clone
  1151.1 6.3 fusion.49
  1157.5 26.9 %convert_multiply_fusion.2 = (f32[16,16,17,512]{3,1,2,0:T(8,128)}, bf16[16,16,17,512]{3,1,2,0:T(8,128)(2,1)S(1)}) fusion(f32[512]{0:T(512)S(1)} %bitcast.330, bf16[4,3,3,512,512]{4,3,2,1,0:T(8,128)(2,1)} %param.14, bf16[18,2,8,19,512]{4,1,3,2,0:T(2,128)(2,1)S(1)} %fusion.49, pred[16,17]{0,1:T(8,128)(4,1)S(1)} %copy-done.25), kind=kOutput, calls=%fused_computation.108 | convolution fusion | flops 20546453504 | bytes 23693584 | tf_op jit(solution)/shard_map/conv_general_dilated | solution.py:29
  1189.8 8.7 copy.91
  1199.2 10.1 psum.39
  1212.0 11.7 multiply_convert_fusion
  1240.0 6.1 maximum_bitcast_fusion.3
  1246.1 9.9 copy.107
  1255.9 9.8 pad.8.clone
  1267.1 6.3 fusion.50
  1273.5 26.4 %select_add_fusion = f32[16,16,17,512]{3,1,2,0:T(8,128)} fusion(bf16[4,3,3,512,512]{4,3,2,1,0:T(8,128)(2,1)} %param.14, bf16[18,2,8,19,512]{4,1,3,2,0:T(2,128)(2,1)S(1)} %fusion.50, f32[512]{0:T(512)S(1)} %bitcast.329, pred[16,17]{0,1:T(8,128)(4,1)S(1)} %copy-done.25), kind=kOutput, calls=%fused_computation.44 | convolution fusion | flops 20539768832 | bytes 19237136 | tf_op jit(solution)/shard_map/conv_general_dilated | solution.py:29
  1299.9 8.8 copy.101
  1312.4 6.5 copy.102
  (222 shorter events, 163.5 us)
Async XLA Ops:
  6.5 20.6 %copy-start = (bf16[3,3,16,512]{3,2,1,0:T(8,128)(2,1)S(1)}, bf16[3,3,16,512]{3,2,1,0:T(8,128)(2,1)}, u32[]{:S(2)}) copy-start(bf16[3,3,16,512]{3,2,1,0:T(8,128)(2,1)} %param.12) | copy-start | bytes 442372
  6.6 20.6 %copy-start.24 = (pred[16,17]{0,1:T(8,128)(4,1)S(1)}, pred[16,17]{0,1:T(8,128)(4,1)}, u32[]{:S(2)}) copy-start(pred[16,17]{0,1:T(8,128)(4,1)} %constant.161) | copy-start | bytes 820
  6.6 475.4 %all-gather.3.cloned.1.call-start = ((), (), s32[]{:S(2)}) async-start(), calls=%async_computation | async-start | bytes 37748736 | tf_op jit(solution)/shard_map/all_gather | solution.py:75
  7.3 13.1 collective-permute-start
  11.9 8.5 collective-permute-start.1
  34.7 2.1 copy-start.5
  81.9 10.5 collective-permute-start.3
  86.1 5.2 collective-permute-start.2
  152.7 2.1 copy-start.7
  198.4 10.5 collective-permute-start.5
  202.7 5.2 collective-permute-start.4
  234.4 8.0 slice-start
  234.4 8.0 copy-start.22
  236.0 6.4 slice-start.1
  269.7 2.1 copy-start.8
  274.4 3.5 copy-start.2
  299.9 2.3 slice-start.2
  299.9 2.3 copy-start.14
  299.9 2.3 copy-start.15
  301.0 1.3 slice-start.3
  318.6 2.9 copy-start.21
  318.7 2.9 copy-start.23
  321.5 4.3 copy-start.9
  321.5 4.4 copy-start.20
  325.9 312.3 %all-gather.5.cloned.1.call-start = ((), (), s32[]{:S(2)}) async-start(), calls=%async_computation.1 | async-start | bytes 37748736 | tf_op jit(solution)/shard_map/all_gather | solution.py:76
  325.9 6.6 copy-start.19
  638.1 443.5 %copy-start.18 = (f32[1,512]{1,0:T(1,128)S(1)}, f32[1,512]{1,0:T(1,128)}, u32[]{:S(2)}) copy-start(f32[1,512]{1,0:T(1,128)} %get-tuple-element.178) | copy-start | bytes 6148
  1081.6 5.0 copy-start.3
  1086.6 19.5 %copy-start.12 = (f32[1,512]{1,0:T(1,128)S(1)}, f32[1,512]{1,0:T(1,128)}, u32[]{:S(2)}) copy-start(f32[1,512]{1,0:T(1,128)} %get-tuple-element.168) | copy-start | bytes 6148
  1086.6 19.5 %copy-start.13 = (f32[1,512]{1,0:T(1,128)S(1)}, f32[1,512]{1,0:T(1,128)}, u32[]{:S(2)}) copy-start(f32[1,512]{1,0:T(1,128)} %get-tuple-element.173) | copy-start | bytes 6148
  1111.4 8.2 collective-permute-start.6
  1113.6 10.5 collective-permute-start.7
  1149.7 7.8 copy-start.17
  1149.7 7.8 copy-start.25
  1184.4 2.1 copy-start.6
  1209.7 2.3 copy-start.10
  1209.7 2.3 copy-start.11
  1229.0 11.0 collective-permute-start.9
  1234.3 5.2 collective-permute-start.8
  1265.7 7.8 copy-start.16
  1299.9 8.8 copy-start.4
  1308.7 10.2 copy-start.1
Sparse Core Ops, SparseCore 0:
  326.0 155.9 all-gather.2
  483.5 154.5 all-gather.4
where the time goes:
time: 1330 us
  matrix products  467 us (35%)
  waiting for transfers between devices  310 us (23%)
  other arithmetic  237 us (18%)
  local copies, waits for them, and re-layouts  208 us (16%)
  blocking collectives  57.9 us (4%)
  starting transfers between devices  30.5 us (2%)
  between operations  14.5 us (1%)
    dot_general x8, matrix products, attend_step(): jnp.dot(attn_prob, v_sample, preferred_element_type=jnp.float32)  171 us
    dot_general x8, matrix products, attend_step(): lax.dot_general(q_block, k_sample, (((1,), (1,)), ((), ())), preferred_el...  159 us
    all_gather x1, waiting for transfers between devices, local_fn(): vals_all = lax.all_gather(project(2), 'cp', axis=1, tiled=True)  156 us
    all_gather x1, waiting for transfers between devices, local_fn(): keys_all = lax.all_gather(project(1), 'cp', axis=1, tiled=True)  143 us
    conv_general_dilated x5, matrix products, conv_rows(): lax.conv_general_dilated(padded, weight, (1, 1), ((0, 0), (1, 1)), dimens...  115 us
    reduce_sum x8, other arithmetic, attend_step(): attn_prob = jax.nn.softmax(scores, axis=-1).astype(jnp.bfloat16)  112 us
    psum x5, blocking collectives, group_norm(): totals = lax.psum(local_sums, 'cp')  57.9 us
    unnamed x65, local copies, waits for them, and re-layouts  51.7 us
  transfers between devices with their start and end apart: 12, of which 9 were waited for; matrix products, arithmetic and copies ran while one was open for 2% of the time, Pallas kernels for 0%

commit v1 on v0

v1 whole, which is shorter than its diff:
```python
import functools

import jax
import jax.numpy as jnp
from jax import lax
from jax.experimental import pallas as pl
from jax.experimental.pallas import tpu as pltpu
from jax.sharding import PartitionSpec as P

GROUPS = 32
GN_EPS = 1e-6
LOG2E = 1.4426950408889634
MESH = pl.DeviceIdType.MESH
F32, BF16 = jnp.float32, jnp.bfloat16
ANY = pl.BlockSpec(memory_space=pl.ANY)
VMEM = pl.BlockSpec(memory_space=pltpu.VMEM)
SMEM = pl.BlockSpec(memory_space=pltpu.SMEM)
MIB = 1024 * 1024


def peer(n_dev, offset):
    return {'cp': lax.rem(lax.axis_index('cp') + 2 * offset + n_dev, n_dev)}


def add_stats(st_ref, yf):
    y3 = yf.reshape(yf.shape[0] // 8, 8, yf.shape[1])
    st_ref[0:8, :] += jnp.sum(y3, axis=0)
    st_ref[8:16, :] += jnp.sum(y3 * y3, axis=0)


def conv_in_kernel(n_blk, p_ref, w_ref, b_ref, y_ref, st_ref):
    m = y_ref.shape[0] // n_blk
    st_ref[...] = jnp.zeros_like(st_ref)

    def body(i, _):
        off = pl.multiple_of(i * m, m)
        acc = lax.dot_general(p_ref[:, pl.ds(off, m)], w_ref[...], (((0,), (0,)), ((), ())), preferred_element_type=F32)
        y = (acc + b_ref[...]).astype(BF16)
        y_ref[pl.ds(off, m), :] = y
        yf = y.astype(F32)
        add_stats(st_ref, yf)
        return 0

    lax.fori_loop(0, n_blk, body, 0)


def conv_in(patches, w2, bias):
    tok, ch = patches.shape[1], w2.shape[1]
    return pl.pallas_call(
        functools.partial(conv_in_kernel, 8),
        out_shape=(jax.ShapeDtypeStruct((tok, ch), BF16), jax.ShapeDtypeStruct((16, ch), F32)),
        in_specs=[VMEM] * 3,
        out_specs=(VMEM, VMEM),
        name='conv_in',
        compiler_params=pltpu.CompilerParams(vmem_limit_bytes=24 * MIB),
    )(patches, w2, bias)


def exchange_kernel(n_dev, count, width, x_ref, st_ref, gain_ref, aff_ref, top_ref, bot_ref, sbuf, send_sem, recv_sem):
    tok = x_ref.shape[0]
    n_chip = n_dev // 2
    barrier = pltpu.get_barrier_semaphore()
    for d in range(1, n_chip):
        pl.semaphore_signal(barrier, inc=1, device_id=peer(n_dev, d), device_id_type=MESH)
    pl.semaphore_wait(barrier, n_chip - 1)
    copies = []
    copies.append(pltpu.make_async_remote_copy(
        x_ref.at[pl.ds(tok - width, width)], top_ref, send_sem.at[0], recv_sem.at[0], device_id=peer(n_dev, 1), device_id_type=MESH))
    copies.append(pltpu.make_async_remote_copy(
        x_ref.at[pl.ds(0, width)], bot_ref, send_sem.at[1], recv_sem.at[1], device_id=peer(n_dev, -1), device_id_type=MESH))
    stats = [pltpu.make_async_remote_copy(
        st_ref, sbuf.at[d - 1], send_sem.at[1 + d], recv_sem.at[1 + d], device_id=peer(n_dev, d), device_id_type=MESH)
        for d in range(1, n_chip)]
    for c in stats + copies:
        c.start()
    tot = st_ref[...]
    for c in stats:
        c.wait()
    for d in range(1, n_chip):
        tot = tot + sbuf[d - 1]
    ch = tot.shape[1]
    lane = lax.broadcasted_iota(jnp.int32, tot.shape, 1)
    k = 1
    while k < ch // GROUPS:
        tot = tot + jnp.where((lane & k) != 0, pltpu.roll(tot, k, 1), pltpu.roll(tot, ch - k, 1))
        k *= 2
    tot = tot * (1.0 / count)
    mean, square = tot[0:8, :], tot[8:16, :]
    for k in (1, 2, 4):
        mean = mean + pltpu.roll(mean, k, 0)
        square = square + pltpu.roll(square, k, 0)
    aff_ref[0:8, :] = mean
    aff_ref[8:16, :] = lax.rsqrt(square - mean * mean + GN_EPS) * gain_ref[0:8, :]
    aff_ref[16:24, :] = gain_ref[8:16, :]
    for c in copies:
        c.wait()


def exchange(n_dev, width, x, st, gain):
    tok, ch = x.shape
    n_chip = n_dev // 2
    count = tok * n_chip * (ch // GROUPS)
    return pl.pallas_call(
        functools.partial(exchange_kernel, n_dev, count, width),
        out_shape=(jax.ShapeDtypeStruct((24, ch), F32), jax.ShapeDtypeStruct((width, ch), BF16), jax.ShapeDtypeStruct((width, ch), BF16)),
        in_specs=[ANY, VMEM, VMEM],
        out_specs=(VMEM, VMEM, VMEM),
        scratch_shapes=[
            pltpu.VMEM((n_chip - 1, 16, ch), F32),
            pltpu.SemaphoreType.DMA((n_chip + 1,)),
            pltpu.SemaphoreType.DMA((n_chip + 1,)),
        ],
        name='exchange',
        compiler_params=pltpu.CompilerParams(collective_id=0, has_side_effects=True, vmem_limit_bytes=8 * MIB),
    )(x, st, gain)


def conv_kernel(width, n_rows, blk_rows, has_res, *refs):
    if has_res:
        (x_ref, top_ref, bot_ref, edge_ref, aff_ref, w_ref, b_ref, r_ref, y_ref, st_ref,
         xs, u3, ws, ys, rs, x_sem, w_sem, y_sem, r_sem) = refs
    else:
        (x_ref, top_ref, bot_ref, edge_ref, aff_ref, w_ref, b_ref, y_ref, st_ref,
         xs, u3, ws, ys, x_sem, w_sem, y_sem) = refs
    ch = x_ref.shape[1]
    n_blk = n_rows // blk_rows
    m = blk_rows * width
    x_in = [pltpu.make_async_copy(x_ref.at[pl.ds(b * m, m)], xs.at[pl.ds(b * m, m)], x_sem.at[b]) for b in range(n_blk)]
    for c in x_in:
        c.start()
    w_in = [pltpu.make_async_copy(w_ref.at[d], ws.at[d], w_sem.at[d]) for d in range(3)]
    for c in w_in:
        c.start()
    if has_res:
        r_in = pltpu.make_async_copy(r_ref, rs, r_sem.at[0])
        r_in.start()
    mean, scale, shift = aff_ref[0:1, :], aff_ref[8:9, :], aff_ref[16:17, :]
    rows = lax.broadcasted_iota(jnp.int32, (width, ch), 0)

    def prep(v, row, keep=None):
        t = (v.astype(F32) - mean) * scale + shift
        u = t / (1.0 + jnp.exp(-t))
        if keep is not None:
            u = jnp.where(keep, u, 0.0)
        off = pl.multiple_of(row * width, width)
        u3[pl.ds(off, width), 0:ch] = jnp.where(rows == 0, 0.0, pltpu.roll(u, 1, 0)).astype(BF16)
        u3[pl.ds(off, width), ch:2 * ch] = u.astype(BF16)
        u3[pl.ds(off, width), 2 * ch:3 * ch] = jnp.where(rows == width - 1, 0.0, pltpu.roll(u, width - 1, 0)).astype(BF16)

    prep(top_ref[...], 0, edge_ref[0] != 0)
    prep(bot_ref[...], n_rows + 1, edge_ref[1] != 0)
    for b in range(n_blk):
        x_in[b].wait()

        def prep_row(i, _):
            row = b * blk_rows + i
            prep(xs[pl.ds(pl.multiple_of(row * width, width), width), :], row + 1)
            return 0

        lax.fori_loop(0, blk_rows, prep_row, 0)
    for c in w_in:
        c.wait()
    if has_res:
        r_in.wait()
    st_ref[...] = jnp.zeros_like(st_ref)

    def block(b, _):
        off = pl.multiple_of(b * m, m)
        acc = jnp.dot(u3[pl.ds(off, m), :], ws[0], preferred_element_type=F32)
        acc += jnp.dot(u3[pl.ds(pl.multiple_of(off + width, width), m), :], ws[1], preferred_element_type=F32)
        acc += jnp.dot(u3[pl.ds(pl.multiple_of(off + 2 * width, width), m), :], ws[2], preferred_element_type=F32)
        acc += b_ref[...]
        if has_res:
            acc += rs[pl.ds(off, m), :].astype(F32)
        y = acc.astype(BF16)
        ys[pl.ds(off, m), :] = y
        yf = y.astype(F32)
        add_stats(st_ref, yf)
        pltpu.make_async_copy(ys.at[pl.ds(off, m)], y_ref.at[pl.ds(off, m)], y_sem.at[b]).start()
        return 0

    lax.fori_loop(0, n_blk, block, 0)
    for b in range(n_blk):
        pltpu.make_async_copy(ys.at[pl.ds(b * m, m)], y_ref.at[pl.ds(b * m, m)], y_sem.at[b]).wait()


def conv(width, x, top, bot, edge, aff, w3, bias, res=None):
    tok, ch = x.shape
    n_rows = tok // width
    blk_rows = 4
    n_blk = n_rows // blk_rows
    has_res = res is not None
    scratch = [
        pltpu.VMEM((tok, ch), BF16),
        pltpu.VMEM((tok + 2 * width, 3 * ch), BF16),
        pltpu.VMEM(w3.shape, BF16),
        pltpu.VMEM((tok, ch), BF16),
    ]
    sems = [pltpu.SemaphoreType.DMA((n_blk,)), pltpu.SemaphoreType.DMA((3,)), pltpu.SemaphoreType.DMA((n_blk,))]
    if has_res:
        scratch.append(pltpu.VMEM((tok, ch), BF16))
        sems.append(pltpu.SemaphoreType.DMA((1,)))
    args = [x, top, bot, edge, aff, w3, bias] + ([res] if has_res else [])
    return pl.pallas_call(
        functools.partial(conv_kernel, width, n_rows, blk_rows, has_res),
        out_shape=(jax.ShapeDtypeStruct((tok, ch), BF16), jax.ShapeDtypeStruct((16, ch), F32)),
        in_specs=[ANY, VMEM, VMEM, SMEM, VMEM, ANY, VMEM] + ([ANY] if has_res else []),
        out_specs=(ANY, VMEM),
        scratch_shapes=scratch + sems,
        name='conv_res' if has_res else 'conv',
        compiler_params=pltpu.CompilerParams(vmem_limit_bytes=48 * MIB),
    )(*args)


def attn_kernel(n_dev, n_chunk, q_blk, q_sub, h_ref, aff_ref, wq_ref, wk_ref, wv_ref, wo_ref, b_ref, y_ref, st_ref,
                nbuf, q_s, acc_s, m_s, l_s, k_s, v_s, send_sem, recv_sem):
    tok, ch = h_ref.shape
    kc = tok // n_chunk
    half = n_chunk // 2
    n_recv = 3 * n_chunk
    scale = ch ** -0.5 * LOG2E
    right, left = peer(n_dev, 1), peer(n_dev, -1)
    barrier = pltpu.get_barrier_semaphore()
    for p in (left, right):
        pl.semaphore_signal(barrier, inc=1, device_id=p, device_id_type=MESH)
    pl.semaphore_wait(barrier, 2)
    sends = []
    for i in range(n_chunk):
        for side, p in ((0, right), (1, left)):
            c = i if side == 0 else (i + half) % n_chunk
            slot = 2 * i + side
            sends.append(pltpu.make_async_remote_copy(
                h_ref.at[pl.ds(c * kc, kc)], nbuf.at[slot], send_sem.at[slot], recv_sem.at[slot], device_id=p, device_id_type=MESH))
    for c in sends:
        c.start()

    def forward(slot):
        return pltpu.make_async_remote_copy(
            nbuf.at[slot], nbuf.at[2 * n_chunk + slot], send_sem.at[2 * n_chunk + slot], recv_sem.at[2 * n_chunk + slot],
            device_id=right if slot % 2 == 0 else left, device_id_type=MESH)

    mean, gain, shift = aff_ref[0:1, :], aff_ref[8:9, :], aff_ref[16:17, :]

    def norm(v):
        return ((v.astype(F32) - mean) * gain + shift).astype(BF16)

    pb = 512

    def project_q(i, _):
        rows = pl.ds(pl.multiple_of(i * pb, pb), pb)
        q_s[rows, :] = (jnp.dot(norm(h_ref[rows, :]), wq_ref[...], preferred_element_type=F32) + b_ref[0:1, :]).astype(BF16)
        acc_s[rows, :] = jnp.zeros((pb, ch), F32)
        m_s[rows, :] = jnp.full((pb, 128), -jnp.inf, F32)
        l_s[rows, :] = jnp.zeros((pb, 128), F32)
        return 0

    lax.fori_loop(0, tok // pb, project_q, 0)

    def step(s, _):
        def project_kv(load):
            def body(i, _):
                rows = pl.ds(pl.multiple_of(i * pb, pb), pb)
                n = norm(load(i * pb))
                k_s[rows, :] = (jnp.dot(n, wk_ref[...], preferred_element_type=F32) + b_ref[1:2, :]).astype(BF16)
                v_s[rows, :] = (jnp.dot(n, wv_ref[...], preferred_element_type=F32) + b_ref[2:3, :]).astype(BF16)
                return 0
            lax.fori_loop(0, kc // pb, body, 0)

        @pl.when(s < n_chunk)
        def _():
            project_kv(lambda o: h_ref[pl.ds(pl.multiple_of(s * kc + o, pb), pb), :])

        @pl.when(s >= n_chunk)
        def _():
            slot = s - n_chunk
            pltpu.make_async_remote_copy(
                nbuf.at[slot], nbuf.at[slot], send_sem.at[slot], recv_sem.at[slot], device_id=right, device_id_type=MESH).wait_recv()
            for f in range(n_chunk):
                @pl.when(slot == f)
                def _():
                    forward(f).start()
            project_kv(lambda o: nbuf[slot, pl.ds(pl.multiple_of(o, pb), pb), :])

        def q_block(i, _):
            n_sub = q_blk // q_sub
            base = i * q_blk
            rows = [pl.ds(pl.multiple_of(base + j * q_sub, q_sub), q_sub) for j in range(n_sub)]

            def score(j):
                return lax.dot_general(q_s[rows[j], :], k_s[...], (((1,), (1,)), ((), ())), preferred_element_type=F32)

            def update(j, sc):
                m_old = m_s[rows[j], :]
                m_new = jnp.maximum(m_old, jnp.max(sc, axis=1, keepdims=True))
                alpha = jnp.exp2((m_old - m_new) * scale)
                p = jnp.exp2((sc - jnp.tile(m_new, (1, kc // 128))) * scale)
                part = p[:, 0:128]
                for t in range(1, kc // 128):
                    part = part + p[:, t * 128:(t + 1) * 128]
                l_s[rows[j], :] = l_s[rows[j], :] * alpha + part
                m_s[rows[j], :] = m_new
                pv = jnp.dot(p.astype(BF16), v_s[...], preferred_element_type=F32)
                acc_s[rows[j], :] = acc_s[rows[j], :] * jnp.tile(alpha, (1, ch // 128)) + pv

            sc = score(0)
            for j in range(n_sub):
                nxt = score(j + 1) if j + 1 < n_sub else None
                update(j, sc)
                sc = nxt
            return 0

        lax.fori_loop(0, tok // q_blk, q_block, 0)
        return 0

    lax.fori_loop(0, n_chunk + n_recv, step, 0)

    st_ref[...] = jnp.zeros_like(st_ref)

    def finish(i, _):
        rows = pl.ds(pl.multiple_of(i * pb, pb), pb)
        o = (acc_s[rows, :] / jnp.sum(l_s[rows, :], axis=1, keepdims=True)).astype(BF16)
        y = (h_ref[rows, :].astype(F32) + (jnp.dot(o, wo_ref[...], preferred_element_type=F32) + b_ref[3:4, :])).astype(BF16)
        y_ref[rows, :] = y
        yf = y.astype(F32)
        add_stats(st_ref, yf)
        return 0

    lax.fori_loop(0, tok // pb, finish, 0)
    for c in sends:
        c.wait_send()
    for f in range(n_chunk):
        forward(f).wait_send()


def attention(n_dev, h, aff, w_attn, b_attn):
    tok, ch = h.shape
    n_chunk = 4
    kc = tok // n_chunk
    n_recv = 3 * n_chunk
    return pl.pallas_call(
        functools.partial(attn_kernel, n_dev, n_chunk, 1024, 256),
        out_shape=(jax.ShapeDtypeStruct((tok, ch), BF16), jax.ShapeDtypeStruct((16, ch), F32)),
        in_specs=[VMEM] * 7,
        out_specs=(VMEM, VMEM),
        scratch_shapes=[
            pltpu.VMEM((n_recv, kc, ch), BF16),
            pltpu.VMEM((tok, ch), BF16),
            pltpu.VMEM((tok, ch), F32),
            pltpu.VMEM((tok, 128), F32),
            pltpu.VMEM((tok, 128), F32),
            pltpu.VMEM((kc, ch), BF16),
            pltpu.VMEM((kc, ch), BF16),
            pltpu.SemaphoreType.DMA((n_recv,)),
            pltpu.SemaphoreType.DMA((n_recv,)),
        ],
        name='attention',
        compiler_params=pltpu.CompilerParams(collective_id=1, has_side_effects=True, vmem_limit_bytes=63 * MIB),
    )(h, aff, w_attn[0], w_attn[1], w_attn[2], w_attn[3], b_attn)


def solution(mesh):
    n_dev = mesh.shape['cp']

    def local_fn(latents, w_in, b_in, w_conv, b_conv, gn_scale, gn_shift, w_attn, b_attn):
        _, band, width, z_ch = latents.shape
        ch = w_in.shape[3]
        n_rows = 2 * band
        tok = n_rows * width
        idx = lax.axis_index('cp')
        core = lax.rem(idx, 2)
        chip = idx // 2
        n_chip = n_dev // 2

        swap = [(i, i ^ 1) for i in range(n_dev)]
        mine = lax.dynamic_index_in_dim(latents, core, 0, keepdims=False)
        other = lax.ppermute(lax.dynamic_index_in_dim(latents, 1 - core, 0, keepdims=False), 'cp', swap)
        down = [lax.ppermute(latents[c, -1:], 'cp', [(2 * i + 1, 2 * (i + 1) + c) for i in range(n_chip - 1)]) for c in range(2)]
        up = [lax.ppermute(latents[c, :1], 'cp', [(2 * (i + 1), 2 * i + c) for i in range(n_chip - 1)]) for c in range(2)]
        first, second = jnp.where(core == 0, mine, other), jnp.where(core == 0, other, mine)
        rows = jnp.concatenate([down[0] + down[1], first, second, up[0] + up[1]], axis=0)
        rows = jnp.pad(jnp.transpose(rows, (2, 0, 1)), ((0, 0), (0, 0), (1, 1)))
        patches = jnp.concatenate([rows[:, dy:dy + n_rows, dx:dx + width] for dy in range(3) for dx in range(3)], axis=0)
        h, st = conv_in(patches.reshape(9 * z_ch, tok), w_in.reshape(9 * z_ch, ch), b_in.astype(F32).reshape(1, ch))

        edge = jnp.stack([chip > 0, chip < n_chip - 1]).astype(jnp.int32)
        gains = jnp.repeat(jnp.stack([gn_scale, gn_shift], axis=1).astype(F32), 8, axis=1)
        w3 = w_conv.reshape(w_conv.shape[0], 3, 3 * ch, ch)
        bc = b_conv.astype(F32)[:, None, :]

        def resnet(h, st, a, g):
            aff, top, bot = exchange(n_dev, width, h, st, gains[g])
            t, st = conv(width, h, top, bot, edge, aff, w3[a], bc[a])
            aff, top, bot = exchange(n_dev, width, t, st, gains[g + 1])
            return conv(width, t, top, bot, edge, aff, w3[a + 1], bc[a + 1], h)

        h, st = resnet(h, st, 0, 0)
        aff, _, _ = exchange(n_dev, width, h, st, gains[2])
        h, st = attention(n_dev, h, aff, w_attn, b_attn.astype(F32))
        h, _ = resnet(h, st, 2, 3)

        h = h.reshape(2, band, width, ch)
        keep = lax.dynamic_index_in_dim(h, core, 0, keepdims=False)
        got = lax.ppermute(lax.dynamic_index_in_dim(h, 1 - core, 0, keepdims=False), 'cp', swap)
        return jnp.stack([jnp.where(core == 0, keep, got), jnp.where(core == 0, got, keep)])

    band_spec = P('dp', 'cp')
    whole_spec = P()
    return jax.shard_map(local_fn, mesh=mesh, in_specs=(band_spec,) + (whole_spec,) * 8, out_specs=band_spec, check_vma=False)
```

time: 1330 us -> 402 us (0.30)
  matrix products: 467 us -> 0 us
  Pallas kernels: 0 us -> 355 us
  waiting for transfers between devices: 310 us -> 3.8 us
  other arithmetic: 237 us -> 4.34 us
  local copies, waits for them, and re-layouts: 208 us -> 21.8 us
  blocking collectives: 57.9 us -> 0 us
  between operations: 14.5 us -> 0.49 us
  starting transfers between devices: 30.5 us -> 16.9 us
    pallas_call x0 -> x11, Pallas kernels: none -> 355 us  [the longest x1 206 us: attention(): pl.pallas_call(functools.partial(attn_kernel, n_dev, n_chunk, 1024, 256),...]
    dot_general x20 -> x0, matrix products: 353 us -> none  [the longest x8 171 us: attend_step(): jnp.dot(attn_prob, v_sample, preferred_element_type=jnp.float32)]
    all_gather x2 -> x0, waiting for transfers between devices: 299 us -> none  [the longest x1 156 us: local_fn(): vals_all = lax.all_gather(project(2), 'cp', axis=1, tiled=True)]
    reduce_sum x27 -> x0, other arithmetic: 124 us -> none  [the longest x8 112 us: attend_step(): attn_prob = jax.nn.softmax(scores, axis=-1).astype(jnp.bfloat16)]
    conv_general_dilated x5 -> x0, matrix products: 115 us -> none  [conv_rows(): lax.conv_general_dilated(padded, weight, (1, 1), ((0, 0), (1, 1)), dimens...]
    convert_element_type x10 -> x3, other arithmetic: 59.8 us -> 1.63 us  [the longest x1 0.95 us: local_fn(): jnp.stack([gn_scale, gn_shift], axis=1).astype(F32)]
    psum x5 -> x0, blocking collectives: 57.9 us -> none  [group_norm(): totals = lax.psum(local_sums, 'cp')]
    convert_element_type x29 -> x0, local copies, waits for them, and re-layouts: 47.7 us -> none  [the longest x14 15.5 us: resnet_block(): jax.nn.silu(group_norm(mid_act, gn_scale[norm_idx + 1], gn_shift[norm_idx...]
  transfers between devices with their start and end apart: 12 -> 6, of which waited for: 9 -> 1; matrix products, arithmetic and copies ran while one was open for 2% -> 4% of each run, Pallas kernels for 0% -> 0%
where the time goes in v1:
time: 402 us
  Pallas kernels  355 us (88%)
  local copies, waits for them, and re-layouts  21.8 us (5%)
  starting transfers between devices  16.9 us (4%)
  other arithmetic  4.34 us (1%)
    pallas_call x1, Pallas kernels, attention(): pl.pallas_call(functools.partial(attn_kernel, n_dev, n_chunk, 1024, 256),...  206 us
    pallas_call x4, Pallas kernels, conv(): pl.pallas_call(functools.partial(conv_kernel, width, n_rows, blk_rows, ha...  113 us
    pallas_call x5, Pallas kernels, exchange(): pl.pallas_call(functools.partial(exchange_kernel, n_dev, count, width), o...  31.5 us
    slice x2, local copies, waits for them, and re-layouts, resnet(): return conv(width, t, top, bot, edge, aff, w3[a + 1], bc[a + 1], h)  14 us
  transfers between devices with their start and end apart: 6, of which 1 were waited for; matrix products, arithmetic and copies ran while one was open for 4% of the time, Pallas kernels for 0%

profile of v1, /device:TPU:81, one launch (start us, length us, event | category | flops | bytes accessed | tf_op | source)
XLA Modules:
  0.0 402.0 jit_solution(10967554168977430890)
XLA Ops:
  0.0 0.8 dynamic-slice_bitcast_fusion.1
  0.8 2.0 collective-permute-start.2
  2.9 0.7 slice_bitcast_fusion.6
  3.6 2.6 collective-permute-start
  6.2 3.3 collective-permute-start.1
  9.5 0.7 collective-permute-start.3
  10.1 1.3 collective-permute-start.4
  11.5 1.0 fusion.8
  12.5 0.0 copy-start.10
  12.5 0.0 copy-start.8
  12.5 14.0 %fusion.9 = (bf16[1,3,3,512,512]{4,3,2,1,0:T(8,128)(2,1)}, bf16[1,3,3,512,512]{4,3,2,1,0:T(8,128)(2,1)}, bf16[1,3,3,512,512]{4,3,2,1,0:T(8,128)(2,1)}, bf16[1,3,3,512,512]{4,3,2,1,0:T(8,128)(2,1)}) fusion(bf16[4,3,3,512,512]{4,3,2,1,0:T(8,128)(2,1)} %param.12), kind=kLoop, calls=%fused_computation.51 | loop fusion | bytes 37748736 | tf_op jit(solution)/shard_map/slice | solution.py:394
  26.5 0.0 copy-done.10
  26.5 0.0 copy-done.8
  26.6 0.0 copy-start.12
  26.6 0.0 copy-start.11
  26.6 0.0 copy-start.9
  26.6 1.4 slice_bitcast_fusion
  28.0 0.1 add_convert_fusion.refs_3_
  28.0 0.0 copy-done.12
  28.1 0.0 copy-done.11
  28.1 0.6 convert_element_type.18.b_ref
  28.7 0.0 collective-permute-done
  28.7 0.0 collective-permute-done.1
  28.7 0.0 collective-permute-done.3
  28.7 0.0 collective-permute-done.4
  28.7 0.0 collective-permute-done.2
  28.7 0.0 copy-done.9
  28.8 0.1 fusion.2
  28.9 0.0 copy-start.5
  28.9 0.1 fusion.3
  29.1 0.1 fusion.4
  29.2 0.1 fusion.5
  29.3 0.1 fusion.6
  29.5 0.1 fusion.7
  29.6 0.1 copy_bitcast_fusion.p_ref
  29.8 0.1 copy-done.5
  29.8 3.4 conv_in.1
  33.2 0.0 copy-start.1
  33.2 7.3 %exchange.5 = (f32[24,512]{1,0:T(8,128)S(1)}, bf16[128,512]{1,0:T(8,128)(2,1)S(1)}, bf16[128,512]{1,0:T(8,128)(2,1)S(1)}) custom-call(bf16[4096,512]{1,0:T(8,128)(2,1)S(1)} %get-tuple-element.29.x_ref.refs_0_.refs_7_, f32[16,512]{1,0:T(8,128)S(1)} %get-tuple-element.30.st_ref, f32[16,512]{1,0:T(8,128)S(1)} %broadcast_bitcast_fusion.4.gain_ref), custom_call_target="tpu_custom_call" | custom-call | tf_op jit(solution)/shard_map/exchange/pallas_call | solution.py:103
  40.5 0.0 copy-done.1
  40.5 27.9 %conv.2 = (bf16[4096,512]{1,0:T(8,128)(2,1)S(1)}, f32[16,512]{1,0:T(8,128)S(1)}) custom-call(bf16[4096,512]{1,0:T(8,128)(2,1)} %copy-done.1, bf16[128,512]{1,0:T(8,128)(2,1)S(1)} %get-tuple-element.31.refs_1_, bf16[128,512]{1,0:T(8,128)(2,1)S(1)} %get-tuple-element.32.refs_2_, s32[2]{0:T(128)S(1)} %add_convert_fusion.refs_3_, ...), custom_call_target="tpu_custom_call" | custom-call | tf_op jit(solution)/shard_map/conv/pallas_call | solution.py:204
  68.5 0.0 copy-start.4
  68.5 5.9 %exchange.6 = (f32[24,512]{1,0:T(8,128)S(1)}, bf16[128,512]{1,0:T(8,128)(2,1)S(1)}, bf16[128,512]{1,0:T(8,128)(2,1)S(1)}) custom-call(bf16[4096,512]{1,0:T(8,128)(2,1)S(1)} %get-tuple-element.34.x_ref.refs_0_, f32[16,512]{1,0:T(8,128)S(1)} %get-tuple-element.35.st_ref, f32[16,512]{1,0:T(8,128)S(1)} %broadcast_bitcast_fusion.3.gain_ref), custom_call_target="tpu_custom_call" | custom-call | tf_op jit(solution)/shard_map/exchange/pallas_call | solution.py:103
  74.4 0.0 copy-done.4
  74.4 28.4 %conv_res.2 = (bf16[4096,512]{1,0:T(8,128)(2,1)S(1)}, f32[16,512]{1,0:T(8,128)S(1)}) custom-call(bf16[4096,512]{1,0:T(8,128)(2,1)} %copy-done.4, bf16[128,512]{1,0:T(8,128)(2,1)S(1)} %get-tuple-element.36.refs_1_, bf16[128,512]{1,0:T(8,128)(2,1)S(1)} %get-tuple-element.37.refs_2_, s32[2]{0:T(128)S(1)} %add_convert_fusion.refs_3_, ...), custom_call_target="tpu_custom_call" | custom-call | tf_op jit(solution)/shard_map/conv_res/pallas_call | solution.py:204
  102.8 0.0 copy-start.2
  102.8 6.6 %exchange.7 = (f32[24,512]{1,0:T(8,128)S(1)}, bf16[128,512]{1,0:T(8,128)(2,1)}, bf16[128,512]{1,0:T(8,128)(2,1)}) custom-call(bf16[4096,512]{1,0:T(8,128)(2,1)S(1)} %get-tuple-element.39.x_ref.h_ref, f32[16,512]{1,0:T(8,128)S(1)} %get-tuple-element.40.st_ref, f32[16,512]{1,0:T(8,128)S(1)} %broadcast_bitcast_fusion.2.gain_ref), custom_call_target="tpu_custom_call" | custom-call | tf_op jit(solution)/shard_map/exchange/pallas_call | solution.py:103
  109.5 0.0 copy-done.2
  109.5 0.0 copy-start.6
  109.5 0.6 copy-done.6
  110.1 206.4 %attention.1 = (bf16[4096,512]{1,0:T(8,128)(2,1)}, f32[16,512]{1,0:T(8,128)}) custom-call(bf16[4096,512]{1,0:T(8,128)(2,1)} %copy-done.2, f32[24,512]{1,0:T(8,128)} %copy-done.6, bf16[512,512]{1,0:T(8,128)(2,1)} %get-tuple-element.61.wq_ref, bf16[512,512]{1,0:T(8,128)(2,1)} %get-tuple-element.60.wk_ref, bf16[512,512]{1,0:T(8,128)(2,1)} %get-tuple-element.62.wv_ref, ...), custom_call_target="tpu_custom_call" | custom-call | tf_op jit(solution)/shard_map/attention/pallas_call | solution.py:340
  316.5 0.0 copy-start
  316.5 2.2 copy-done
  318.7 0.8 copy-done.7
  319.5 5.9 %exchange.8 = (f32[24,512]{1,0:T(8,128)S(1)}, bf16[128,512]{1,0:T(8,128)(2,1)S(1)}, bf16[128,512]{1,0:T(8,128)(2,1)S(1)}) custom-call(bf16[4096,512]{1,0:T(8,128)(2,1)S(1)} %copy-done, f32[16,512]{1,0:T(8,128)S(1)} %copy-done.7, f32[16,512]{1,0:T(8,128)S(1)} %broadcast_bitcast_fusion.1.gain_ref), custom_call_target="tpu_custom_call" | custom-call | tf_op jit(solution)/shard_map/exchange/pallas_call | solution.py:103
  325.3 28.0 %conv.3 = (bf16[4096,512]{1,0:T(8,128)(2,1)S(1)}, f32[16,512]{1,0:T(8,128)S(1)}) custom-call(bf16[4096,512]{1,0:T(8,128)(2,1)} %get-tuple-element.42.x_ref.refs_0_.refs_7_, bf16[128,512]{1,0:T(8,128)(2,1)S(1)} %get-tuple-element.44.refs_1_, bf16[128,512]{1,0:T(8,128)(2,1)S(1)} %get-tuple-element.45.refs_2_, s32[2]{0:T(128)S(1)} %add_convert_fusion.refs_3_, ...), custom_call_target="tpu_custom_call" | custom-call | tf_op jit(solution)/shard_map/conv/pallas_call | solution.py:204
  353.3 0.0 copy-start.3
  353.3 5.9 %exchange.9 = (f32[24,512]{1,0:T(8,128)S(1)}, bf16[128,512]{1,0:T(8,128)(2,1)S(1)}, bf16[128,512]{1,0:T(8,128)(2,1)S(1)}) custom-call(bf16[4096,512]{1,0:T(8,128)(2,1)S(1)} %get-tuple-element.47.x_ref.refs_0_, f32[16,512]{1,0:T(8,128)S(1)} %get-tuple-element.48.st_ref, f32[16,512]{1,0:T(8,128)S(1)} %broadcast_bitcast_fusion.gain_ref), custom_call_target="tpu_custom_call" | custom-call | tf_op jit(solution)/shard_map/exchange/pallas_call | solution.py:103
  359.2 29.0 %conv_res.3 = (bf16[4096,512]{1,0:T(8,128)(2,1)S(1)}, f32[16,512]{1,0:T(8,128)}) custom-call(bf16[4096,512]{1,0:T(8,128)(2,1)} %copy-done.3, bf16[128,512]{1,0:T(8,128)(2,1)S(1)} %get-tuple-element.49.refs_1_, bf16[128,512]{1,0:T(8,128)(2,1)S(1)} %get-tuple-element.50.refs_2_, s32[2]{0:T(128)S(1)} %add_convert_fusion.refs_3_, ...), custom_call_target="tpu_custom_call" | custom-call | tf_op jit(solution)/shard_map/conv_res/pallas_call | solution.py:204
  388.2 0.2 dynamic-slice_bitcast_fusion
  388.5 7.1 %collective-permute-start.5 = (bf16[16,128,512]{2,1,0:T(8,128)(2,1)S(1)}, bf16[16,128,512]{2,1,0:T(8,128)(2,1)S(1)}, u32[]{:S(2)}, u32[]{:S(2)}) collective-permute-start(bf16[16,128,512]{2,1,0:T(8,128)(2,1)S(1)} %dynamic-slice_bitcast_fusion), channel_id=1, source_target_pairs={{0,1},{1,0},{2,3},{3,2},{4,5},{5,4},{6,7},{7,6},{8,9},{9,8},{10,11... | collective-permute-start | bytes 6291464 | tf_op jit(solution)/shard_map/ppermute | solution.py:403
  395.6 3.8 collective-permute-done.5
  399.4 0.3 fusion
  399.6 2.4 pad_maximum_fusion
  (19 shorter events, 0.2 us)
Async XLA Ops:
  0.8 27.9 %collective-permute-start.2 = (bf16[16,128,16]{1,2,0:T(8,128)(2,1)S(1)}, bf16[16,128,16]{1,2,0:T(8,128)(2,1)S(1)}, u32[]{:S(2)}, u32[]{:S(2)}) collective-permute-start(bf16[16,128,16]{1,2,0:T(8,128)(2,1)S(1)} %dynamic-slice_bitcast_fusion.1), channel_id=1, source_target_pairs={{0,1},{1,0},{2,3},{3,2},{4,5},{5,4},{6,7},{7,6},{8,9},{9,8},{10,11... | collective-permute-start | bytes 196616 | tf_op jit(solution)/shard_map/ppermute | solution.py:376
  3.6 25.0 %collective-permute-start = (bf16[1,128,16]{1,2,0:T(8,128)(2,1)S(1)}, bf16[1,128,16]{1,2,0:T(8,128)(2,1)S(1)}, u32[]{:S(2)}, u32[]{:S(2)}) collective-permute-start(bf16[1,128,16]{1,2,0:T(8,128)(2,1)S(1)} %get-tuple-element.66), channel_id=1, source_target_pairs={{1,2},{3,4},{5,6},{9,10},{11,12},{13,14},{17,18},{19,20},{21,22},{... | collective-permute-start | bytes 12296 | tf_op jit(solution)/shard_map/ppermute | solution.py:377
  6.2 22.5 %collective-permute-start.1 = (bf16[1,128,16]{1,2,0:T(8,128)(2,1)S(1)}, bf16[1,128,16]{1,2,0:T(8,128)(2,1)S(1)}, u32[]{:S(2)}, u32[]{:S(2)}) collective-permute-start(bf16[1,128,16]{1,2,0:T(8,128)(2,1)S(1)} %get-tuple-element.65), channel_id=1, source_target_pairs={{1,3},{3,5},{5,7},{9,11},{11,13},{13,15},{17,19},{19,21},{21,23},{... | collective-permute-start | bytes 12296 | tf_op jit(solution)/shard_map/ppermute | solution.py:377
  9.5 19.2 %collective-permute-start.3 = (bf16[1,128,16]{1,2,0:T(8,128)(2,1)S(1)}, bf16[1,128,16]{1,2,0:T(8,128)(2,1)S(1)}, u32[]{:S(2)}, u32[]{:S(2)}) collective-permute-start(bf16[1,128,16]{1,2,0:T(8,128)(2,1)S(1)} %get-tuple-element.68), channel_id=1, source_target_pairs={{2,0},{4,2},{6,4},{10,8},{12,10},{14,12},{18,16},{20,18},{22,20},{... | collective-permute-start | bytes 12296 | tf_op jit(solution)/shard_map/ppermute | solution.py:378
  10.1 18.5 %collective-permute-start.4 = (bf16[1,128,16]{1,2,0:T(8,128)(2,1)S(1)}, bf16[1,128,16]{1,2,0:T(8,128)(2,1)S(1)}, u32[]{:S(2)}, u32[]{:S(2)}) collective-permute-start(bf16[1,128,16]{1,2,0:T(8,128)(2,1)S(1)} %get-tuple-element.67), channel_id=1, source_target_pairs={{2,1},{4,3},{6,5},{10,9},{12,11},{14,13},{18,17},{20,19},{22,21},{... | collective-permute-start | bytes 12296 | tf_op jit(solution)/shard_map/ppermute | solution.py:378
  12.5 14.0 %copy-start.10 = (bf16[4,512]{1,0:T(4,128)(2,1)S(1)}, bf16[4,512]{1,0:T(4,128)(2,1)}, u32[]{:S(2)}) copy-start(bf16[4,512]{1,0:T(4,128)(2,1)} %param.13) | copy-start | bytes 12292
  12.5 14.1 %copy-start.8 = (bf16[4,512,512]{2,1,0:T(8,128)(2,1)S(1)}, bf16[4,512,512]{2,1,0:T(8,128)(2,1)}, u32[]{:S(2)}) copy-start(bf16[4,512,512]{2,1,0:T(8,128)(2,1)} %param.16) | copy-start | bytes 6291460
  26.6 1.5 copy-start.12
  26.6 1.5 copy-start.11
  26.6 2.1 copy-start.9
  28.9 0.9 copy-start.5
  33.2 7.3 %copy-start.1 = (bf16[4096,512]{1,0:T(8,128)(2,1)}, bf16[4096,512]{1,0:T(8,128)(2,1)S(1)}, u32[]{:S(2)}) copy-start(bf16[4096,512]{1,0:T(8,128)(2,1)S(1)} %get-tuple-element.29.x_ref.refs_0_.refs_7_) | copy-start | bytes 12582916
  68.5 5.9 %copy-start.4 = (bf16[4096,512]{1,0:T(8,128)(2,1)}, bf16[4096,512]{1,0:T(8,128)(2,1)S(1)}, u32[]{:S(2)}) copy-start(bf16[4096,512]{1,0:T(8,128)(2,1)S(1)} %get-tuple-element.34.x_ref.refs_0_) | copy-start | bytes 12582916
  102.8 6.6 %copy-start.2 = (bf16[4096,512]{1,0:T(8,128)(2,1)}, bf16[4096,512]{1,0:T(8,128)(2,1)S(1)}, u32[]{:S(2)}) copy-start(bf16[4096,512]{1,0:T(8,128)(2,1)S(1)} %get-tuple-element.39.x_ref.h_ref) | copy-start | bytes 12582916
  109.5 0.6 copy-start.6
  316.5 2.2 copy-start
  318.7 0.8 copy-start.7
  353.3 5.9 %copy-start.3 = (bf16[4096,512]{1,0:T(8,128)(2,1)}, bf16[4096,512]{1,0:T(8,128)(2,1)S(1)}, u32[]{:S(2)}) copy-start(bf16[4096,512]{1,0:T(8,128)(2,1)S(1)} %get-tuple-element.47.x_ref.refs_0_) | copy-start | bytes 12582916
  388.5 10.9 %collective-permute-start.5 = (bf16[16,128,512]{2,1,0:T(8,128)(2,1)S(1)}, bf16[16,128,512]{2,1,0:T(8,128)(2,1)S(1)}, u32[]{:S(2)}, u32[]{:S(2)}) collective-permute-start(bf16[16,128,512]{2,1,0:T(8,128)(2,1)S(1)} %dynamic-slice_bitcast_fusion), channel_id=1, source_target_pairs={{0,1},{1,0},{2,3},{3,2},{4,5},{5,4},{6,7},{7,6},{8,9},{9,8},{10,11... | collective-permute-start | bytes 6291464 | tf_op jit(solution)/shard_map/ppermute | solution.py:403

commit v2 on v1

v2 whole, which is shorter than its diff:
```python
import functools

import jax
import jax.numpy as jnp
from jax import lax
from jax.experimental import pallas as pl
from jax.experimental.pallas import tpu as pltpu
from jax.sharding import PartitionSpec as P

GROUPS = 32
GN_EPS = 1e-6
LOG2E = 1.4426950408889634
MESH = pl.DeviceIdType.MESH
F32, BF16 = jnp.float32, jnp.bfloat16
ANY = pl.BlockSpec(memory_space=pl.ANY)
VMEM = pl.BlockSpec(memory_space=pltpu.VMEM)
SMEM = pl.BlockSpec(memory_space=pltpu.SMEM)
MIB = 1024 * 1024


def peer(n_dev, offset):
    return {'cp': lax.rem(lax.axis_index('cp') + 2 * offset + n_dev, n_dev)}


def add_stats(st_s, yf):
    y3 = yf.reshape(yf.shape[0] // 8, 8, yf.shape[1])
    st_s[0:8, :] += jnp.sum(y3, axis=0)
    st_s[8:16, :] += jnp.sum(y3 * y3, axis=0)


def fold_stats(st_s):
    a, b = st_s[0:8, :], st_s[8:16, :]
    row = lax.broadcasted_iota(jnp.int32, a.shape, 0)
    return jnp.where(row < 4, a + pltpu.roll(a, 4, 0), b + pltpu.roll(b, 4, 0))


def conv_in_kernel(n_blk, width, z_ref, w_ref, b_ref, y_ref, st_ref, p_s, st_s):
    tok = y_ref.shape[0]
    z_ch, span = z_ref.shape
    m = tok // n_blk
    z = z_ref[...].astype(F32)
    col = lax.rem(lax.broadcasted_iota(jnp.int32, z.shape, 1), width)
    taps = [jnp.where(col == 0, 0.0, pltpu.roll(z, 1, 1)), z, jnp.where(col == width - 1, 0.0, pltpu.roll(z, span - 1, 1))]
    for dx in range(3):
        tap = taps[dx].astype(BF16)
        for dy in range(3):
            k = (3 * dy + dx) * z_ch
            p_s[k:k + z_ch, :] = tap[:, dy * width:dy * width + tok]
    st_s[...] = jnp.zeros_like(st_s)

    def body(i, _):
        off = pl.multiple_of(i * m, m)
        acc = lax.dot_general(p_s[:, pl.ds(off, m)], w_ref[...], (((0,), (0,)), ((), ())), preferred_element_type=F32)
        y = (acc + b_ref[...]).astype(BF16)
        y_ref[pl.ds(off, m), :] = y
        add_stats(st_s, y.astype(F32))
        return 0

    lax.fori_loop(0, n_blk, body, 0)
    st_ref[...] = fold_stats(st_s)


def conv_in(width, z, w2, bias):
    tok, ch = z.shape[1] - 2 * width, w2.shape[1]
    return pl.pallas_call(
        functools.partial(conv_in_kernel, 8, width),
        out_shape=(jax.ShapeDtypeStruct((tok, ch), BF16), jax.ShapeDtypeStruct((8, ch), F32)),
        in_specs=[VMEM] * 3,
        out_specs=(VMEM, VMEM),
        scratch_shapes=[pltpu.VMEM((w2.shape[0], tok), BF16), pltpu.VMEM((16, ch), F32)],
        name='conv_in',
        compiler_params=pltpu.CompilerParams(vmem_limit_bytes=24 * MIB),
    )(z, w2, bias)


def greet_peers(n_dev):
    barrier = pltpu.get_barrier_semaphore()
    for d in range(1, n_dev // 2):
        pl.semaphore_signal(barrier, inc=1, device_id=peer(n_dev, d), device_id_type=MESH)


def await_peers(n_dev):
    pl.semaphore_wait(pltpu.get_barrier_semaphore(), n_dev // 2 - 1)


def share_scratch(n_dev, ch):
    n_peer = n_dev // 2 - 1
    return [pltpu.VMEM((n_peer, 8, ch), F32), pltpu.SemaphoreType.DMA((n_peer,)), pltpu.SemaphoreType.DMA((n_peer,))]


def exchange_kernel(n_dev, count, st_ref, gain_ref, aff_ref, sbuf, send_sem, recv_sem):
    greet_peers(n_dev)
    await_peers(n_dev)
    share_stats(n_dev, count, st_ref, gain_ref, aff_ref, sbuf, send_sem, recv_sem)


def share_stats(n_dev, count, st_ref, gain_ref, aff_ref, sbuf, send_sem, recv_sem):
    n_chip = n_dev // 2
    copies = [pltpu.make_async_remote_copy(
        st_ref, sbuf.at[d - 1], send_sem.at[d - 1], recv_sem.at[d - 1], device_id=peer(n_dev, d), device_id_type=MESH)
        for d in range(1, n_chip)]
    for c in copies:
        c.start()
    tot = st_ref[...]
    for c in copies:
        c.wait()
    for d in range(1, n_chip):
        tot = tot + sbuf[d - 1]
    ch = tot.shape[1]
    row = lax.broadcasted_iota(jnp.int32, tot.shape, 0)
    lane = lax.broadcasted_iota(jnp.int32, tot.shape, 1)
    for k in (1, 2):
        tot = tot + jnp.where((row & k) != 0, pltpu.roll(tot, k, 0), pltpu.roll(tot, 8 - k, 0))
    k = 1
    while k < ch // GROUPS:
        tot = tot + jnp.where((lane & k) != 0, pltpu.roll(tot, k, 1), pltpu.roll(tot, ch - k, 1))
        k *= 2
    tot = tot * (1.0 / count)
    flip = pltpu.roll(tot, 4, 0)
    mean, square = jnp.where(row < 4, tot, flip), jnp.where(row < 4, flip, tot)
    aff_ref[0:8, :] = mean
    aff_ref[8:16, :] = lax.rsqrt(square - mean * mean + GN_EPS) * gain_ref[0:8, :]
    aff_ref[16:24, :] = gain_ref[8:16, :]


def exchange(n_dev, tok, st, gain):
    ch = st.shape[1]
    n_chip = n_dev // 2
    count = tok * n_chip * (ch // GROUPS)
    return pl.pallas_call(
        functools.partial(exchange_kernel, n_dev, count),
        out_shape=jax.ShapeDtypeStruct((24, ch), F32),
        in_specs=[VMEM, VMEM],
        out_specs=VMEM,
        scratch_shapes=share_scratch(n_dev, ch),
        name='exchange',
        compiler_params=pltpu.CompilerParams(collective_id=0, has_side_effects=True, vmem_limit_bytes=8 * MIB),
    )(st, gain)


def conv_kernel(n_dev, width, n_rows, blk_rows, which, has_res, share, count, *refs):
    refs = list(refs)

    def take(n):
        got = refs[:n]
        del refs[:n]
        return got

    x_ref, aff_ref, w_ref, b_ref = take(4)
    r_ref, = take(1) if has_res else (None,)
    gain_ref, = take(1) if share else (None,)
    y_ref, = take(1)
    out_aff_ref, = take(1) if share else (None,)
    xs, ua, ub, ws, ys, st_s, own, x_sem, w_sem, y_sem, send_sem, recv_sem = take(12)
    rs, r_sem = take(2) if has_res else (None, None)
    tok, ch = x_ref.shape
    n_blk = n_rows // blk_rows
    m = blk_rows * width
    right, left = peer(n_dev, 1), peer(n_dev, -1)
    greet_peers(n_dev)
    x_in = [pltpu.make_async_copy(x_ref.at[pl.ds(b * m, m)], xs.at[pl.ds(width + b * m, m)], x_sem.at[b]) for b in range(n_blk)]
    for c in x_in:
        c.start()
    w_in = [pltpu.make_async_copy(w_ref.at[which, d], ws.at[d], w_sem.at[d]) for d in range(3)]
    for c in w_in:
        c.start()
    if has_res:
        r_in = pltpu.make_async_copy(r_ref, rs, r_sem.at[0])
        r_in.start()
    await_peers(n_dev)
    halos = [
        pltpu.make_async_remote_copy(x_ref.at[pl.ds(tok - width, width)], xs.at[pl.ds(0, width)],
                                     send_sem.at[0], recv_sem.at[0], device_id=right, device_id_type=MESH),
        pltpu.make_async_remote_copy(x_ref.at[pl.ds(0, width)], xs.at[pl.ds(width + tok, width)],
                                     send_sem.at[1], recv_sem.at[1], device_id=left, device_id_type=MESH),
    ]
    for c in halos:
        c.start()
    st_s[...] = jnp.zeros_like(st_s)
    mean, scale, shift = aff_ref[0:1, :], aff_ref[8:9, :], aff_ref[16:17, :]
    chip = lax.axis_index('cp') // 2
    has_top, has_bot = chip > 0, chip < n_dev // 2 - 1
    cols = lax.broadcasted_iota(jnp.int32, (width, ch), 0)

    def block_of(j):
        return lax.rem(j + 1, n_blk)

    def prep(u3, b):
        for r in range(blk_rows + 2):
            v = xs[pl.ds(pl.multiple_of((b * blk_rows + r) * width, width), width), :]
            t = (v.astype(F32) - mean) * scale + shift
            u = t / (1.0 + jnp.exp(-t))
            if r == 0:
                u = jnp.where(jnp.logical_or(b > 0, has_top), u, 0.0)
            if r == blk_rows + 1:
                u = jnp.where(jnp.logical_or(b < n_blk - 1, has_bot), u, 0.0)
            rows = slice(r * width, (r + 1) * width)
            u3[rows, 0:ch] = jnp.where(cols == 0, 0.0, pltpu.roll(u, 1, 0)).astype(BF16)
            u3[rows, ch:2 * ch] = u.astype(BF16)
            u3[rows, 2 * ch:3 * ch] = jnp.where(cols == width - 1, 0.0, pltpu.roll(u, width - 1, 0)).astype(BF16)

    def dots(u3, b):
        off = pl.multiple_of(b * m, m)
        acc = jnp.dot(u3[0:m, :], ws[0], preferred_element_type=F32)
        acc += jnp.dot(u3[width:width + m, :], ws[1], preferred_element_type=F32)
        acc += jnp.dot(u3[2 * width:2 * width + m, :], ws[2], preferred_element_type=F32)
        acc += b_ref[...]
        if has_res:
            acc += rs[pl.ds(off, m), :].astype(F32)
        y = acc.astype(BF16)
        ys[pl.ds(off, m), :] = y
        if share:
            add_stats(st_s, y.astype(F32))
        pltpu.make_async_copy(ys.at[pl.ds(off, m)], y_ref.at[pl.ds(off, m)], y_sem.at[b]).start()

    for c in x_in[:3]:
        c.wait()
    prep(ua, 1)
    for c in x_in[3:]:
        c.wait()
    for c in w_in:
        c.wait()
    if has_res:
        r_in.wait()

    def pair(i, _):
        @pl.when(i == n_blk // 2 - 2)
        def _():
            for c in halos:
                c.wait_recv()

        j = 2 * i
        dots(ua, block_of(j))
        prep(ub, block_of(j + 1))
        dots(ub, block_of(j + 1))
        prep(ua, block_of(j + 2))
        return 0

    lax.fori_loop(0, n_blk // 2, pair, 0)
    own[...] = fold_stats(st_s)
    for c in halos:
        c.wait_send()
    for b in range(n_blk):
        pltpu.make_async_copy(ys.at[pl.ds(b * m, m)], y_ref.at[pl.ds(b * m, m)], y_sem.at[b]).wait()
    if share:
        share_stats(n_dev, count, own, gain_ref, out_aff_ref, *refs)


def conv(n_dev, width, x, aff, w3, which, bias, res=None, gain=None):
    tok, ch = x.shape
    n_rows = tok // width
    blk_rows = 4
    n_blk = n_rows // blk_rows
    has_res, share = res is not None, gain is not None
    count = tok * (n_dev // 2) * (ch // GROUPS)
    scratch = [
        pltpu.VMEM((tok + 2 * width, ch), BF16),
        pltpu.VMEM(((blk_rows + 2) * width, 3 * ch), BF16),
        pltpu.VMEM(((blk_rows + 2) * width, 3 * ch), BF16),
        pltpu.VMEM(w3.shape[1:], BF16),
        pltpu.VMEM((tok, ch), BF16),
        pltpu.VMEM((16, ch), F32),
        pltpu.VMEM((8, ch), F32),
        pltpu.SemaphoreType.DMA((n_blk,)),
        pltpu.SemaphoreType.DMA((3,)),
        pltpu.SemaphoreType.DMA((n_blk,)),
        pltpu.SemaphoreType.DMA((2,)),
        pltpu.SemaphoreType.DMA((2,)),
    ]
    if has_res:
        scratch += [pltpu.VMEM((tok, ch), BF16), pltpu.SemaphoreType.DMA((1,))]
    if share:
        scratch += share_scratch(n_dev, ch)
    args = [x, aff, w3, bias] + ([res] if has_res else []) + ([gain] if share else [])
    out = pl.pallas_call(
        functools.partial(conv_kernel, n_dev, width, n_rows, blk_rows, which, has_res, share, count),
        out_shape=[jax.ShapeDtypeStruct((tok, ch), BF16)] + ([jax.ShapeDtypeStruct((24, ch), F32)] if share else []),
        in_specs=[ANY, VMEM, ANY, VMEM] + ([ANY] if has_res else []) + ([VMEM] if share else []),
        out_specs=[ANY] + ([VMEM] if share else []),
        scratch_shapes=scratch,
        name=f'conv_{which}',
        compiler_params=pltpu.CompilerParams(
            collective_id=2 + which, has_side_effects=True, vmem_limit_bytes=63 * MIB),
    )(*args)
    return out if share else out[0]


def attn_kernel(n_dev, n_chunk, q_blk, q_sub, count, h_ref, aff_ref, w_ref, b_ref, gain_ref, y_ref, out_aff_ref,
                nbuf, q_s, acc_s, m_s, l_s, k_s, v_s, ys, st_s, own, send_sem, recv_sem, y_sem, *share_refs):
    tok, ch = h_ref.shape
    kc = tok // n_chunk
    half = n_chunk // 2
    n_recv = 3 * n_chunk
    scale = ch ** -0.5 * LOG2E
    right, left = peer(n_dev, 1), peer(n_dev, -1)
    greet_peers(n_dev)
    await_peers(n_dev)
    sends = []
    for i in range(n_chunk):
        for side, p in ((0, right), (1, left)):
            c = i if side == 0 else (i + half) % n_chunk
            slot = 2 * i + side
            sends.append(pltpu.make_async_remote_copy(
                h_ref.at[pl.ds(c * kc, kc)], nbuf.at[slot], send_sem.at[slot], recv_sem.at[slot], device_id=p, device_id_type=MESH))

    def forward(slot):
        return pltpu.make_async_remote_copy(
            nbuf.at[slot], nbuf.at[2 * n_chunk + slot], send_sem.at[2 * n_chunk + slot], recv_sem.at[2 * n_chunk + slot],
            device_id=right if slot % 2 == 0 else left, device_id_type=MESH)

    events = {0: sends[0:2], 1: sends[2:4]}
    for i in range(2, n_chunk):
        events[2 * i - 1] = sends[2 * i:2 * i + 2]
    for i in range(half):
        events[2 * n_chunk - 1 + 2 * i] = [forward(2 * i), forward(2 * i + 1)]

    mean, gain, shift = aff_ref[0:1, :], aff_ref[8:9, :], aff_ref[16:17, :]

    def norm(v):
        return ((v.astype(F32) - mean) * gain + shift).astype(BF16)

    pb = min(512, kc)
    for c in events[0]:
        c.start()

    def project_q(i, _):
        rows = pl.ds(pl.multiple_of(i * pb, pb), pb)
        q_s[rows, :] = (jnp.dot(norm(h_ref[rows, :]), w_ref[0], preferred_element_type=F32) + b_ref[0:1, :]).astype(BF16)
        acc_s[rows, :] = jnp.zeros((pb, ch), F32)
        m_s[rows, :] = jnp.full((pb, 128), -jnp.inf, F32)
        l_s[rows, :] = jnp.zeros((pb, 128), F32)
        return 0

    lax.fori_loop(0, tok // pb, project_q, 0)

    def step(s, _):
        for at, group in events.items():
            if at == 0:
                continue

            @pl.when(s == at)
            def _():
                for c in group:
                    c.start()

        def project_kv(load):
            def body(i, _):
                rows = pl.ds(pl.multiple_of(i * pb, pb), pb)
                n = norm(load(i * pb))
                k_s[rows, :] = (jnp.dot(n, w_ref[1], preferred_element_type=F32) + b_ref[1:2, :]).astype(BF16)
                v_s[rows, :] = (jnp.dot(n, w_ref[2], preferred_element_type=F32) + b_ref[2:3, :]).astype(BF16)
                return 0
            lax.fori_loop(0, kc // pb, body, 0)

        @pl.when(s < n_chunk)
        def _():
            project_kv(lambda o: h_ref[pl.ds(pl.multiple_of(s * kc + o, pb), pb), :])

        @pl.when(s >= n_chunk)
        def _():
            slot = s - n_chunk
            pltpu.make_async_remote_copy(
                nbuf.at[slot], nbuf.at[slot], send_sem.at[slot], recv_sem.at[slot], device_id=right, device_id_type=MESH).wait_recv()
            project_kv(lambda o: nbuf[slot, pl.ds(pl.multiple_of(o, pb), pb), :])

        def q_block(i, _):
            n_sub = q_blk // q_sub
            base = i * q_blk
            rows = [pl.ds(pl.multiple_of(base + j * q_sub, q_sub), q_sub) for j in range(n_sub)]

            def score(j):
                return lax.dot_general(q_s[rows[j], :], k_s[...], (((1,), (1,)), ((), ())), preferred_element_type=F32)

            def update(j, sc):
                m_old = m_s[rows[j], :]
                m_new = jnp.maximum(m_old, jnp.max(sc, axis=1, keepdims=True))
                alpha = jnp.exp2((m_old - m_new) * scale)
                p = jnp.exp2((sc - jnp.tile(m_new, (1, kc // 128))) * scale)
                part = p[:, 0:128]
                for t in range(1, kc // 128):
                    part = part + p[:, t * 128:(t + 1) * 128]
                l_s[rows[j], :] = l_s[rows[j], :] * alpha + part
                m_s[rows[j], :] = m_new
                pv = jnp.dot(p.astype(BF16), v_s[...], preferred_element_type=F32)
                acc_s[rows[j], :] = acc_s[rows[j], :] * jnp.tile(alpha, (1, ch // 128)) + pv

            sc = score(0)
            for j in range(n_sub):
                nxt = score(j + 1) if j + 1 < n_sub else None
                update(j, sc)
                sc = nxt
            return 0

        lax.fori_loop(0, tok // q_blk, q_block, 0)
        return 0

    lax.fori_loop(0, n_chunk + n_recv, step, 0)

    st_s[...] = jnp.zeros_like(st_s)

    def finish(i, _):
        rows = pl.ds(pl.multiple_of(i * pb, pb), pb)
        o = (acc_s[rows, :] / jnp.sum(l_s[rows, :], axis=1, keepdims=True)).astype(BF16)
        y = (h_ref[rows, :].astype(F32) + (jnp.dot(o, w_ref[3], preferred_element_type=F32) + b_ref[3:4, :])).astype(BF16)
        ys[rows, :] = y
        add_stats(st_s, y.astype(F32))
        pltpu.make_async_copy(ys.at[rows], y_ref.at[rows], y_sem.at[i]).start()
        return 0

    lax.fori_loop(0, tok // pb, finish, 0)
    own[...] = fold_stats(st_s)
    for i in range(tok // pb):
        rows = pl.ds(i * pb, pb)
        pltpu.make_async_copy(ys.at[rows], y_ref.at[rows], y_sem.at[i]).wait()
    for c in sends:
        c.wait_send()
    for f in range(n_chunk):
        forward(f).wait_send()
    share_stats(n_dev, count, own, gain_ref, out_aff_ref, *share_refs)


def attention(n_dev, h, aff, w_attn, b_attn, gain):
    tok, ch = h.shape
    n_chunk = 4
    kc = tok // n_chunk
    n_recv = 3 * n_chunk
    return pl.pallas_call(
        functools.partial(attn_kernel, n_dev, n_chunk, 1024, 512, tok * (n_dev // 2) * (ch // GROUPS)),
        out_shape=(jax.ShapeDtypeStruct((tok, ch), BF16), jax.ShapeDtypeStruct((24, ch), F32)),
        in_specs=[VMEM] * 5,
        out_specs=(ANY, VMEM),
        scratch_shapes=[
            pltpu.VMEM((n_recv, kc, ch), BF16),
            pltpu.VMEM((tok, ch), BF16),
            pltpu.VMEM((tok, ch), F32),
            pltpu.VMEM((tok, 128), F32),
            pltpu.VMEM((tok, 128), F32),
            pltpu.VMEM((kc, ch), BF16),
            pltpu.VMEM((kc, ch), BF16),
            pltpu.VMEM((tok, ch), BF16),
            pltpu.VMEM((16, ch), F32),
            pltpu.VMEM((8, ch), F32),
            pltpu.SemaphoreType.DMA((n_recv,)),
            pltpu.SemaphoreType.DMA((n_recv,)),
            pltpu.SemaphoreType.DMA((tok // min(512, kc),)),
        ] + share_scratch(n_dev, ch),
        name='attention',
        compiler_params=pltpu.CompilerParams(collective_id=1, has_side_effects=True, vmem_limit_bytes=63 * MIB),
    )(h, aff, w_attn, b_attn, gain)


def solution(mesh):
    n_dev = mesh.shape['cp']

    def local_fn(latents, w_in, b_in, w_conv, b_conv, gn_scale, gn_shift, w_attn, b_attn):
        _, band, width, z_ch = latents.shape
        ch = w_in.shape[3]
        n_rows = 2 * band
        tok = n_rows * width
        idx = lax.axis_index('cp')
        core = lax.rem(idx, 2)
        n_chip = n_dev // 2

        swap = [(i, i ^ 1) for i in range(n_dev)]
        mine = lax.dynamic_index_in_dim(latents, core, 0, keepdims=False)
        other = lax.ppermute(lax.dynamic_index_in_dim(latents, 1 - core, 0, keepdims=False), 'cp', swap)
        down = [lax.ppermute(latents[c, -1:], 'cp', [(2 * i + 1, 2 * (i + 1) + c) for i in range(n_chip - 1)]) for c in range(2)]
        up = [lax.ppermute(latents[c, :1], 'cp', [(2 * (i + 1), 2 * i + c) for i in range(n_chip - 1)]) for c in range(2)]
        first, second = jnp.where(core == 0, mine, other), jnp.where(core == 0, other, mine)
        rows = jnp.concatenate([down[0] + down[1], first, second, up[0] + up[1]], axis=0)
        z = jnp.transpose(rows.reshape(tok + 2 * width, z_ch), (1, 0))
        h, st = conv_in(width, z, w_in.reshape(9 * z_ch, ch), b_in.astype(F32).reshape(1, ch))

        gains = jnp.repeat(jnp.stack([gn_scale, gn_shift], axis=1).astype(F32), 8, axis=1)
        w3 = w_conv.reshape(w_conv.shape[0], 3, 3 * ch, ch)
        bc = b_conv.astype(F32)[:, None, :]

        def resnet(h, aff, a, g, gain=None):
            t, aff = conv(n_dev, width, h, aff, w3, a, bc[a], None, gains[g + 1])
            return conv(n_dev, width, t, aff, w3, a + 1, bc[a + 1], h, gain)

        aff = exchange(n_dev, tok, st, gains[0])
        h, aff = resnet(h, aff, 0, 0, gains[2])
        h, aff = attention(n_dev, h, aff, w_attn, b_attn.astype(F32), gains[3])
        h = resnet(h, aff, 2, 3)

        h = h.reshape(2, band, width, ch)
        keep = lax.dynamic_index_in_dim(h, core, 0, keepdims=False)
        got = lax.ppermute(lax.dynamic_index_in_dim(h, 1 - core, 0, keepdims=False), 'cp', swap)
        return jnp.stack([jnp.where(core == 0, keep, got), jnp.where(core == 0, got, keep)])

    band_spec = P('dp', 'cp')
    whole_spec = P()
    return jax.shard_map(local_fn, mesh=mesh, in_specs=(band_spec,) + (whole_spec,) * 8, out_specs=band_spec, check_vma=False)
```

time: 402 us -> 377 us (0.938)
  Pallas kernels: 355 us -> 338 us
  local copies, waits for them, and re-layouts: 21.8 us -> 10.9 us
    pallas_call x11 -> x7, Pallas kernels: 355 us -> 338 us  [the longest x1 204 us: attention(): pl.pallas_call(functools.partial(attn_kernel, n_dev, n_chunk, 1024, 512,...]
    slice x2 -> x1, local copies, waits for them, and re-layouts: 14 us -> 1.43 us  [resnet(): return conv(n_dev, width, t, aff, w3, a + 1, bc[a + 1], h, gain)]
  transfers between devices with their start and end apart: 6 -> 6, of which waited for: 1 -> 1; matrix products, arithmetic and copies ran while one was open for 4% -> 2% of each run, Pallas kernels for 0% -> 0%
where the time goes in v2:
time: 377 us; the launch traced here: 376 us
  Pallas kernels  338 us (90%)
  starting transfers between devices  17.5 us (5%)
  local copies, waits for them, and re-layouts  10.9 us (3%)
  other arithmetic  6.46 us (2%)
  waiting for transfers between devices  3.8 us (1%)
    pallas_call x1, Pallas kernels, attention(): pl.pallas_call(functools.partial(attn_kernel, n_dev, n_chunk, 1024, 512,...  204 us
    pallas_call x4, Pallas kernels, conv(): pl.pallas_call(functools.partial(conv_kernel, n_dev, width, n_rows, blk_r...  125 us
    ppermute x1, starting transfers between devices, local_fn(): lax.ppermute(lax.dynamic_index_in_dim(h, 1 - core, 0, keepdims=False), 'c...  7.62 us
  transfers between devices with their start and end apart: 6, of which 1 were waited for; matrix products, arithmetic and copies ran while one was open for 2% of the time, Pallas kernels for 0%

profile of v2, /device:TPU:81, one launch (start us, length us, event | category | flops | bytes accessed | tf_op | source)
XLA Modules:
  0.0 376.4 jit_solution(3820712762778938103)
XLA Ops:
  0.0 0.8 dynamic-slice_bitcast_fusion.1
  0.8 2.0 collective-permute-start.2
  2.9 0.7 slice_bitcast_fusion.2
  3.6 2.6 collective-permute-start
  6.2 3.3 collective-permute-start.1
  9.5 0.7 collective-permute-start.3
  10.1 1.3 collective-permute-start.4
  11.5 1.0 fusion.2
  12.5 0.6 broadcast_bitcast_fusion.3.refs_4_
  13.1 0.6 broadcast_bitcast_fusion.2.refs_5_
  13.7 0.6 broadcast_bitcast_fusion.1.gain_ref
  14.3 0.6 broadcast_bitcast_fusion.refs_4_
  14.9 1.4 fusion.3
  16.3 0.7 reshape.52
  17.0 1.3 convert_element_type.12.b_ref
  18.3 0.0 collective-permute-done
  18.3 0.0 collective-permute-done.1
  18.3 0.0 collective-permute-done.3
  18.3 0.0 collective-permute-done.4
  18.3 0.0 collective-permute-done.2
  18.3 0.9 bitcast_select_fusion.3
  19.2 0.0 copy-start.2
  19.2 0.9 copy-done.2
  20.1 3.5 conv_in.1
  23.7 0.0 copy-start
  23.7 2.0 copy-done
  25.7 5.0 %exchange.1.refs_1_ = f32[24,512]{1,0:T(8,128)S(1)} custom-call(f32[8,512]{1,0:T(8,128)S(1)} %get-tuple-element.16.st_ref, f32[16,512]{1,0:T(8,128)S(1)} %broadcast_bitcast_fusion.4.gain_ref), custom_call_target="tpu_custom_call" | custom-call | tf_op jit(solution)/shard_map/exchange/pallas_call | solution.py:130
  30.7 0.0 copy-start.1
  30.7 0.6 copy-done.1
  31.3 31.4 %conv_0.1 = (bf16[4096,512]{1,0:T(8,128)(2,1)}, f32[24,512]{1,0:T(8,128)}) custom-call(bf16[4096,512]{1,0:T(8,128)(2,1)} %copy-done, f32[24,512]{1,0:T(8,128)} %copy-done.1, bf16[4,3,1536,512]{3,2,1,0:T(8,128)(2,1)} %bitcast.62, f32[1,512]{1,0:T(1,128)} %get-tuple-element.41.refs_3_, f32[16,512]{1,0:T(8,128)} %broadcast_bitcast_fusion.3.refs_4_), custom_call_target="tpu_custom_call" | custom-call | tf_op jit(solution)/shard_map/conv_0/pallas_call | solution.py:275
  62.7 33.5 %conv_1.1 = (bf16[4096,512]{1,0:T(8,128)(2,1)}, f32[24,512]{1,0:T(8,128)}) custom-call(bf16[4096,512]{1,0:T(8,128)(2,1)} %get-tuple-element.17.refs_0_, f32[24,512]{1,0:T(8,128)} %get-tuple-element.18.refs_1_, bf16[4,3,1536,512]{3,2,1,0:T(8,128)(2,1)} %bitcast.63, f32[1,512]{1,0:T(1,128)} %get-tuple-element.40.refs_3_, bf16[4096,512]{1,0:T(8,128)(2,1)} %copy-done, ...), custom_call_target="tpu_custom_call" | custom-call | tf_op jit(solution)/shard_map/conv_1/pallas_call | solution.py:275
  96.2 204.4 %attention.1 = (bf16[4096,512]{1,0:T(8,128)(2,1)}, f32[24,512]{1,0:T(8,128)}) custom-call(bf16[4096,512]{1,0:T(8,128)(2,1)} %get-tuple-element.19.h_ref, f32[24,512]{1,0:T(8,128)} %get-tuple-element.20.aff_ref, bf16[4,512,512]{2,1,0:T(8,128)(2,1)} %w_ref.1, f32[4,512]{1,0:T(4,128)} %convert_element_type.12.b_ref, f32[16,512]{1,0:T(8,128)} %broadcast_bitcast_fusion.1.gain_ref), custom_call_target="tpu_custom_call" | custom-call | tf_op jit(solution)/shard_map/attention/pallas_call | solution.py:427
  300.6 31.4 %conv_2.1 = (bf16[4096,512]{1,0:T(8,128)(2,1)}, f32[24,512]{1,0:T(8,128)}) custom-call(bf16[4096,512]{1,0:T(8,128)(2,1)} %get-tuple-element.21.refs_0_.refs_4_, f32[24,512]{1,0:T(8,128)} %get-tuple-element.22.refs_1_, bf16[4,3,1536,512]{3,2,1,0:T(8,128)(2,1)} %bitcast.64, f32[1,512]{1,0:T(1,128)} %get-tuple-element.39.refs_3_, ...), custom_call_target="tpu_custom_call" | custom-call | tf_op jit(solution)/shard_map/conv_2/pallas_call | solution.py:275
  332.0 28.4 %conv_3.1 = bf16[4096,512]{1,0:T(8,128)(2,1)} custom-call(bf16[4096,512]{1,0:T(8,128)(2,1)} %get-tuple-element.23.refs_0_, f32[24,512]{1,0:T(8,128)} %get-tuple-element.24.refs_1_, bf16[4,3,1536,512]{3,2,1,0:T(8,128)(2,1)} %bitcast.65, f32[1,512]{1,0:T(1,128)} %get-tuple-element.38.refs_3_, bf16[4096,512]{1,0:T(8,128)(2,1)} %get-tuple-element.21.refs_0_.refs_4_), custom_call_target="tpu_custom_call" | custom-call | tf_op jit(solution)/shard_map/conv_3/pallas_call | solution.py:275
  360.4 0.0 copy-start.3
  360.5 1.9 dynamic-slice_bitcast_fusion
  362.3 7.6 %collective-permute-start.5 = (bf16[16,128,512]{2,1,0:T(8,128)(2,1)S(1)}, bf16[16,128,512]{2,1,0:T(8,128)(2,1)S(1)}, u32[]{:S(2)}, u32[]{:S(2)}) collective-permute-start(bf16[16,128,512]{2,1,0:T(8,128)(2,1)S(1)} %dynamic-slice_bitcast_fusion), channel_id=1, source_target_pairs={{0,1},{1,0},{2,3},{3,2},{4,5},{5,4},{6,7},{7,6},{8,9},{9,8},{10,11... | collective-permute-start | bytes 6291464 | tf_op jit(solution)/shard_map/ppermute | solution.py:489
  370.0 3.8 %collective-permute-done.5 = bf16[16,128,512]{2,1,0:T(8,128)(2,1)S(1)} collective-permute-done((bf16[16,128,512]{2,1,0:T(8,128)(2,1)S(1)}, bf16[16,128,512]{2,1,0:T(8,128)(2,1)S(1)}, u32[]{:S(2)}, u32[]{:S(2)}) %collective-permute-start.5) | collective-permute-done | bytes 2097184 | tf_op jit(solution)/shard_map/ppermute | solution.py:489
  373.8 0.0 copy-done.3
  373.8 0.3 fusion
  374.0 2.4 pad_maximum_fusion
  (7 shorter events, 0.0 us)
Async XLA Ops:
  0.8 17.5 %collective-permute-start.2 = (bf16[16,128,16]{1,2,0:T(8,128)(2,1)S(1)}, bf16[16,128,16]{1,2,0:T(8,128)(2,1)S(1)}, u32[]{:S(2)}, u32[]{:S(2)}) collective-permute-start(bf16[16,128,16]{1,2,0:T(8,128)(2,1)S(1)} %dynamic-slice_bitcast_fusion.1), channel_id=1, source_target_pairs={{0,1},{1,0},{2,3},{3,2},{4,5},{5,4},{6,7},{7,6},{8,9},{9,8},{10,11... | collective-permute-start | bytes 196616 | tf_op jit(solution)/shard_map/ppermute | solution.py:466
  3.6 14.7 %collective-permute-start = (bf16[1,128,16]{1,2,0:T(8,128)(2,1)S(1)}, bf16[1,128,16]{1,2,0:T(8,128)(2,1)S(1)}, u32[]{:S(2)}, u32[]{:S(2)}) collective-permute-start(bf16[1,128,16]{1,2,0:T(8,128)(2,1)S(1)} %get-tuple-element.30), channel_id=1, source_target_pairs={{1,2},{3,4},{5,6},{9,10},{11,12},{13,14},{17,18},{19,20},{21,22},{... | collective-permute-start | bytes 12296 | tf_op jit(solution)/shard_map/ppermute | solution.py:467
  6.2 12.1 %collective-permute-start.1 = (bf16[1,128,16]{1,2,0:T(8,128)(2,1)S(1)}, bf16[1,128,16]{1,2,0:T(8,128)(2,1)S(1)}, u32[]{:S(2)}, u32[]{:S(2)}) collective-permute-start(bf16[1,128,16]{1,2,0:T(8,128)(2,1)S(1)} %get-tuple-element.29), channel_id=1, source_target_pairs={{1,3},{3,5},{5,7},{9,11},{11,13},{13,15},{17,19},{19,21},{21,23},{... | collective-permute-start | bytes 12296 | tf_op jit(solution)/shard_map/ppermute | solution.py:467
  9.5 8.8 %collective-permute-start.3 = (bf16[1,128,16]{1,2,0:T(8,128)(2,1)S(1)}, bf16[1,128,16]{1,2,0:T(8,128)(2,1)S(1)}, u32[]{:S(2)}, u32[]{:S(2)}) collective-permute-start(bf16[1,128,16]{1,2,0:T(8,128)(2,1)S(1)} %get-tuple-element.32), channel_id=1, source_target_pairs={{2,0},{4,2},{6,4},{10,8},{12,10},{14,12},{18,16},{20,18},{22,20},{... | collective-permute-start | bytes 12296 | tf_op jit(solution)/shard_map/ppermute | solution.py:468
  10.1 8.2 %collective-permute-start.4 = (bf16[1,128,16]{1,2,0:T(8,128)(2,1)S(1)}, bf16[1,128,16]{1,2,0:T(8,128)(2,1)S(1)}, u32[]{:S(2)}, u32[]{:S(2)}) collective-permute-start(bf16[1,128,16]{1,2,0:T(8,128)(2,1)S(1)} %get-tuple-element.31), channel_id=1, source_target_pairs={{2,1},{4,3},{6,5},{10,9},{12,11},{14,13},{18,17},{20,19},{22,21},{... | collective-permute-start | bytes 12296 | tf_op jit(solution)/shard_map/ppermute | solution.py:468
  19.2 0.9 copy-start.2
  23.7 2.0 copy-start
  30.7 0.6 copy-start.1
  360.4 13.3 %copy-start.3 = (bf16[4096,512]{1,0:T(8,128)(2,1)S(1)}, bf16[4096,512]{1,0:T(8,128)(2,1)}, u32[]{:S(2)}) copy-start(bf16[4096,512]{1,0:T(8,128)(2,1)} %conv_3.1) | copy-start | bytes 12582916
  362.3 11.4 %collective-permute-start.5 = (bf16[16,128,512]{2,1,0:T(8,128)(2,1)S(1)}, bf16[16,128,512]{2,1,0:T(8,128)(2,1)S(1)}, u32[]{:S(2)}, u32[]{:S(2)}) collective-permute-start(bf16[16,128,512]{2,1,0:T(8,128)(2,1)S(1)} %dynamic-slice_bitcast_fusion), channel_id=1, source_target_pairs={{0,1},{1,0},{2,3},{3,2},{4,5},{5,4},{6,7},{7,6},{8,9},{9,8},{10,11... | collective-permute-start | bytes 6291464 | tf_op jit(solution)/shard_map/ppermute | solution.py:489
